TPU v7x, 8 devices: a whole 2x2x1 slice. The times are simulated.
8 devices in a mesh: dp: 1 (over z), sp: 2 (over y), tp: 4 (over x, core).
Axes of the slice: x: 2, y: 2, z: 1, core: 2. Of those that a mesh axis runs over, the one named last changes fastest.
Arguments:
- x_in: bfloat16 [64, 128, 32, 256], P('dp', 'sp', None, 'tp')
- act_saved: bfloat16 [64, 128, 32, 256], P('dp', 'sp', None, 'tp')
- w_one: bfloat16 [3, 3, 256, 256], P(None, None, 'tp')
- w_two: bfloat16 [3, 3, 256, 256], P(None, None, 'tp')
- d_out: bfloat16 [64, 128, 32, 256], P('dp', 'sp', None, 'tp')
Outputs:
- output 1: bfloat16 [64, 128, 32, 256], P('dp', 'sp', None, 'tp')
- output 2: float32 [3, 3, 256, 256], P('dp', None, 'tp')
- output 3: float32 [3, 3, 256, 256], P('dp', None, 'tp')
- output 4: float32 [256], P(('dp', 'tp'))
All inputs are finite; a program needn't handle non-finite values.
Results may differ from a plain program's by a relative error of at most 0.001.
Values are sent between devices in bfloat16 or wider.
A program may use at most 1 GiB of HBM per device.

v0:
```python
import jax
import jax.numpy as jnp
from jax import lax
from jax.sharding import PartitionSpec as P


def conv_rows(padded, kernel):
    return lax.conv_general_dilated(padded, kernel[::-1, ::-1], (1, 1), ((0, 0), (1, 1)), dimension_numbers=("NHWC", "HWOI", "NHWC"), preferred_element_type=jnp.float32)


def weight_grad(padded, image):
    corr = lax.conv_general_dilated(padded, image, (1, 1), ((0, 0), (1, 1)), dimension_numbers=("CHWN", "IHWO", "HWCN"), preferred_element_type=jnp.float32)
    return corr[::-1, ::-1]


def solution(mesh):
    row_devs = mesh.shape["sp"]
    to_next = [(dev_index, dev_index + 1) for dev_index in range(row_devs - 1)]
    to_prev = [(dev_index + 1, dev_index) for dev_index in range(row_devs - 1)]

    def with_halo(tile):
        above = lax.ppermute(tile[:, -1:], "sp", to_next)
        below = lax.ppermute(tile[:, :1], "sp", to_prev)
        return jnp.concatenate([above, tile, below], axis=1)

    def local_step(x_in, act_saved, w_one, w_two, d_out):
        dy_pad = lax.all_gather(with_halo(d_out), "tp", axis=3, tiled=True)
        d_act = conv_rows(dy_pad, w_two)
        grad_two = lax.psum(weight_grad(dy_pad, act_saved), "sp")
        masked = jnp.where(act_saved > 0, d_act, 0.0)
        grad_bias = lax.psum(jnp.sum(masked, axis=(0, 1, 2)), "sp")
        dz_pad = lax.all_gather(with_halo(masked.astype(jnp.bfloat16)), "tp", axis=3, tiled=True)
        d_x = (d_out.astype(jnp.float32) + conv_rows(dz_pad, w_one)).astype(jnp.bfloat16)
        grad_one = lax.psum(weight_grad(dz_pad, x_in), "sp")
        return d_x, grad_one, grad_two, grad_bias

    act_spec = P("dp", "sp", None, "tp")
    kern_spec = P(None, None, "tp", None)
    grad_spec = P("dp", None, "tp", None)
    return jax.shard_map(local_step, mesh=mesh, in_specs=(act_spec, act_spec, kern_spec, kern_spec, act_spec), out_specs=(act_spec, grad_spec, grad_spec, P(("dp", "tp"))), check_vma=False)
```

profile of v0, /device:TPU:0, one launch (start us, length us, event | category | flops | bytes accessed | tf_op | source)
XLA Modules:
  0.0 2740.9 jit_solution(15831007839884760981)
XLA Ops:
  7.2 0.0 copy-start
  7.2 0.0 all-gather.3.cloned.1.call-start
  7.2 1.3 fusion.7
  8.6 1.3 collective-permute-start.1
  9.9 5.3 collective-permute-start
  15.2 56.7 %copy.33 = bf16[64,64,32,64]{1,2,0,3:T(8,128)(2,1)} copy(bf16[64,64,32,64]{3,2,1,0:T(8,128)(2,1)} %param.9) | data formatting | bytes 33554432 | tf_op args[4]
  71.9 0.0 collective-permute-done.1
  71.9 22.4 copy.34
  94.2 0.0 collective-permute-done
  94.3 23.1 copy.32
  117.4 43.8 %pad_maximum_fusion.1 = bf16[64,66,32,64]{1,2,0,3:T(8,128)(2,1)} fusion(bf16[64,1,32,64]{1,2,0,3:T(8,128)(2,1)} %copy.34, bf16[64,64,32,64]{1,2,0,3:T(8,128)(2,1)} %copy.33, bf16[64,1,32,64]{1,2,0,3:T(8,128)(2,1)} %copy.32), kind=kLoop, calls=%fused_computation.5 | loop fusion | flops 51904512 | bytes 34603008 | tf_op jit(solution)/shard_map/concatenate | solution.py:24
  161.1 0.0 all-gather.3.cloned.1.call-update
  161.1 0.2 all-gather.5.cloned.1.call-start
  161.4 771.4 %all-gather.3.cloned.1.call-done = bf16[64,66,32,256]{1,2,0,3:T(8,128)(2,1)} async-done(((bf16[64,66,32,64]{1,2,0,3:T(8,128)(2,1)}), bf16[64,66,32,256]{1,2,0,3:T(8,128)(2,1)}) %all-gather.3.cloned.1.call-update) | async-done | bytes 69206032 | tf_op jit(solution)/shard_map/all_gather | solution.py:27
  932.8 219.7 %copy.35 = bf16[64,66,32,256]{3,0,2,1:T(8,128)(2,1)} copy(bf16[64,66,32,256]{1,2,0,3:T(8,128)(2,1)} %all-gather.3.cloned.1.call-done) | data formatting | bytes 138412032 | tf_op jit(solution)/shard_map/all_gather | solution.py:27
  1152.4 0.0 copy-done
  1152.4 175.0 %fusion.1 = (bf16[64,64,32,64]{3,0,2,1:T(8,128)(2,1)}, f32[64,64,32,64]{3,0,2,1:T(8,128)}) fusion(bf16[64,64,32,64]{3,2,1,0:T(8,128)(2,1)} %param.6, bf16[64,66,32,256]{3,0,2,1:T(8,128)(2,1)} %copy.35, bf16[3,3,64,256]{3,2,1,0:T(8,128)(2,1)S(1)} %copy-done), kind=kOutput, calls=%fused_computation.3 | convolution fusion | flops 37882953728 | bytes 136609792 | tf_op jit(solution)/shard_map/conv_general_dilated | solution.py:8
  1327.4 1.3 fusion.6
  1328.7 3.4 collective-permute-start.2
  1332.1 1.7 collective-permute-start.3
  1333.8 9.8 collective-permute-done.2
  1343.6 4.2 collective-permute-done.3
  1347.8 23.5 pad_maximum_fusion
  1371.3 66.4 %copy.36 = bf16[64,66,32,64]{1,2,0,3:T(8,128)(2,1)} copy(bf16[64,66,32,64]{3,0,2,1:T(8,128)(2,1)} %pad_maximum_fusion) | data formatting | bytes 34603008 | tf_op jit(solution)/shard_map/concatenate | solution.py:24
  1437.8 0.0 all-gather.5.cloned.1.call-update
  1437.8 0.0 all-reduce.3.cloned.1.call-start
  1437.8 112.8 %fusion.4 = f32[3,3,64,256]{3,2,1,0:T(8,128)S(1)} fusion(bf16[64,66,32,256]{3,0,2,1:T(8,128)(2,1)} %copy.35, bf16[64,64,32,64]{3,2,1,0:T(8,128)(2,1)} %param.6), kind=kOutput, calls=%fused_computation.8 | convolution fusion | flops 37849399296 | bytes 86573056 | tf_op jit(solution)/shard_map/conv_general_dilated | solution.py:12
  1550.7 0.9 rev.9
  1551.5 31.9 %fusion = f32[64]{0:T(128)S(1)} fusion(f32[64,64,32,64]{3,0,2,1:T(8,128)} %get-tuple-element.23, bf16[64,64,32,64]{3,2,1,0:T(8,128)(2,1)} %param.6), kind=kLoop, calls=%fused_computation.2 | loop fusion | flops 25165760 | bytes 50331904 | tf_op jit(solution)/shard_map/reduce_sum | solution.py:31
  1583.4 5.4 psum.23
  1588.9 618.5 %all-gather.5.cloned.1.call-done = bf16[64,66,32,256]{1,2,0,3:T(8,128)(2,1)} async-done(((bf16[64,66,32,64]{1,2,0,3:T(8,128)(2,1)}), bf16[64,66,32,256]{1,2,0,3:T(8,128)(2,1)}) %all-gather.5.cloned.1.call-update) | async-done | bytes 69206032 | tf_op jit(solution)/shard_map/all_gather | solution.py:32
  2207.3 219.7 %copy.37 = bf16[64,66,32,256]{3,0,2,1:T(8,128)(2,1)} copy(bf16[64,66,32,256]{1,2,0,3:T(8,128)(2,1)} %all-gather.5.cloned.1.call-done) | data formatting | bytes 138412032 | tf_op jit(solution)/shard_map/all_gather | solution.py:32
  2427.0 0.0 copy-start.2
  2427.0 112.7 %fusion.2 = f32[3,3,64,256]{3,2,1,0:T(8,128)S(1)} fusion(bf16[64,66,32,256]{3,0,2,1:T(8,128)(2,1)} %copy.37, bf16[64,64,32,64]{3,2,1,0:T(8,128)(2,1)} %param.5), kind=kOutput, calls=%fused_computation.6 | convolution fusion | flops 37849399296 | bytes 86573056 | tf_op jit(solution)/shard_map/conv_general_dilated | solution.py:12
  2539.8 0.9 rev.8
  2540.7 0.0 all-reduce.3.cloned.1.call-update
  2540.7 0.0 copy-done.2
  2540.7 0.0 copy-start.1
  2540.7 166.3 %add_convert_fusion = bf16[64,64,32,64]{3,0,2,1:T(8,128)(2,1)} fusion(bf16[64,64,32,64]{3,2,1,0:T(8,128)(2,1)} %param.9, bf16[64,66,32,256]{3,0,2,1:T(8,128)(2,1)} %copy.37, bf16[3,3,64,256]{3,2,1,0:T(8,128)(2,1)S(1)} %copy-done.2), kind=kOutput, calls=%fused_computation | convolution fusion | flops 37874565120 | bytes 103055360 | tf_op jit(solution)/shard_map/conv_general_dilated | solution.py:8
  2707.0 23.3 copy.42
  2730.3 0.0 all-reduce.3.cloned.1.call-done
  2730.3 1.9 copy.52
  2732.2 1.9 copy.53
  2734.1 0.0 copy-done.1
Async XLA Ops:
  7.2 1145.3 %copy-start = (bf16[3,3,64,256]{3,2,1,0:T(8,128)(2,1)S(1)}, bf16[3,3,64,256]{3,2,1,0:T(8,128)(2,1)}, u32[]{:S(2)}) copy-start(bf16[3,3,64,256]{3,2,1,0:T(8,128)(2,1)} %param.8) | copy-start | bytes 884740
  7.2 925.6 %all-gather.3.cloned.1.call-start = ((), (), s32[]{:S(2)}) async-start(), calls=%async_computation | async-start | bytes 167772160 | tf_op jit(solution)/shard_map/all_gather | solution.py:27
  8.6 63.3 %collective-permute-start.1 = (bf16[64,1,32,64]{3,2,1,0:T(8,128)(2,1)S(1)}, bf16[64,1,32,64]{3,2,1,0:T(8,128)(2,1)S(1)}, u32[]{:S(2)}, u32[]{:S(2)}) collective-permute-start(bf16[64,1,32,64]{3,2,1,0:T(8,128)(2,1)S(1)} %get-tuple-element.21), channel_id=1, source_target_pairs={{4,0},{5,1},{6,2},{7,3}} | collective-permute-start | bytes 786440 | tf_op jit(solution)/shard_map/ppermute | solution.py:23
  9.9 84.4 %collective-permute-start = (bf16[64,1,32,64]{3,2,1,0:T(8,128)(2,1)S(1)}, bf16[64,1,32,64]{3,2,1,0:T(8,128)(2,1)S(1)}, u32[]{:S(2)}, u32[]{:S(2)}) collective-permute-start(bf16[64,1,32,64]{3,2,1,0:T(8,128)(2,1)S(1)} %get-tuple-element.20), channel_id=1, source_target_pairs={{0,4},{1,5},{2,6},{3,7}} | collective-permute-start | bytes 786440 | tf_op jit(solution)/shard_map/ppermute | solution.py:22
  161.1 2046.2 %all-gather.5.cloned.1.call-start = ((), (), s32[]{:S(2)}) async-start(), calls=%async_computation.1 | async-start | bytes 167772160 | tf_op jit(solution)/shard_map/all_gather | solution.py:32
  1328.7 14.9 collective-permute-start.2
  1332.1 15.7 collective-permute-start.3
  1437.8 1292.5 %all-reduce.3.cloned.1.call-start = ((), (), s32[]{:S(2)}) async-start(), calls=%async_computation.2 | async-start | bytes 2359296 | tf_op jit(solution)/shard_map/psum | solution.py:34
  2427.0 113.6 %copy-start.2 = (bf16[3,3,64,256]{3,2,1,0:T(8,128)(2,1)S(1)}, bf16[3,3,64,256]{3,2,1,0:T(8,128)(2,1)}, u32[]{:S(2)}) copy-start(bf16[3,3,64,256]{3,2,1,0:T(8,128)(2,1)} %param.7) | copy-start | bytes 884740
  2540.7 193.4 %copy-start.1 = (bf16[3,3,64,256]{3,2,1,0:T(8,128)(2,1)S(1)}, bf16[3,3,64,256]{3,2,1,0:T(8,128)(2,1)}, u32[]{:S(2)}) copy-start(bf16[3,3,64,256]{3,2,1,0:T(8,128)(2,1)} %param.8) | copy-start | bytes 884740
Sparse Core Ops, SparseCore 0:
  161.3 771.4 all-gather.2
  1437.9 769.3 all-gather.4
  2540.8 37.1 all-reduce.2
where the time goes:
time: 2750 us; the launch traced here: 2740 us
  waiting for transfers between devices  1400 us (51%)
  local copies, waits for them, and re-layouts  639 us (23%)
  matrix products  567 us (21%)
  other arithmetic  99.2 us (4%)
    all_gather x1, waiting for transfers between devices, local_step(): dy_pad = lax.all_gather(with_halo(d_out), 'tp', axis=3, tiled=True)  771 us
    all_gather x1, waiting for transfers between devices, local_step(): lax.all_gather(with_halo(masked.astype(jnp.bfloat16)), 'tp', axis=3, tile...  618 us
    conv_general_dilated x2, matrix products, conv_rows(): lax.conv_general_dilated(padded, kernel[::-1, ::-1], (1, 1), ((0, 0), (1,...  341 us
    conv_general_dilated x2, matrix products, weight_grad(): lax.conv_general_dilated(padded, image, (1, 1), ((0, 0), (1, 1)), dimensi...  226 us
    all_gather x1, local copies, waits for them, and re-layouts, local_step(): dy_pad = lax.all_gather(with_halo(d_out), 'tp', axis=3, tiled=True)  220 us
    all_gather x1, local copies, waits for them, and re-layouts, local_step(): lax.all_gather(with_halo(masked.astype(jnp.bfloat16)), 'tp', axis=3, tile...  220 us
    unnamed x10, local copies, waits for them, and re-layouts  83.8 us
    concatenate x2, other arithmetic, with_halo(): return jnp.concatenate([above, tile, below], axis=1)  67.3 us
  transfers between devices with their start and end apart: 7, of which 4 were waited for; matrix products, arithmetic and copies ran while one was open for 15% of the time, Pallas kernels for 0%

commit v1 on v0

v1 whole, which is shorter than its diff:
```python
import jax
import jax.numpy as jnp
from jax import lax
from jax.experimental import pallas as pl
from jax.experimental.pallas import tpu as pltpu
from jax.sharding import PartitionSpec as P

MESH = pl.DeviceIdType.MESH
F32, BF16 = jnp.float32, jnp.bfloat16
TAPS = 9
CONV_ROWS = 16
GRAD_ROWS = 32


def body(num, rows, width, x_hbm, a_hbm, y_hbm, w1_ref, w2_ref, dx_hbm, acc1, acc2, db_ref,
         nat_own, nat_rem, g_own, g_oth, z_own, z_oth, shifted, out_own, out_rem,
         load_sem, push_send, push_recv, g_send, g_recv, z_send, z_recv, out_sem, out_send, out_recv, free_sem):
    dp, sp, tp = lax.axis_index("dp"), lax.axis_index("sp"), lax.axis_index("tp")
    core = tp % 2
    partner = (dp, sp, tp + 1 - 2 * core)
    across = (dp, sp, (tp + 2) % 4)
    beside = (dp, 1 - sp, tp)
    diagonal = (dp, 1 - sp, (tp + 2) % 4)
    peers = (partner, across, beside, diagonal)
    half = 64
    lanes = 2 * half
    edge_row = (rows + 1) * sp
    halo_row = (rows + 1) * (1 - sp)
    halo_src = rows - (rows - 1) * sp
    m_conv = CONV_ROWS * width
    m_grad = GRAD_ROWS * width

    barrier = pltpu.get_barrier_semaphore()
    for peer in peers:
        pl.semaphore_signal(barrier, inc=1, device_id=peer, device_id_type=MESH)
    pl.semaphore_wait(barrier, 4)

    def remote(src, dst, send, recv, peer):
        return pltpu.make_async_remote_copy(src_ref=src, dst_ref=dst, send_sem=send, recv_sem=recv, device_id=peer, device_id_type=MESH)

    sources = (y_hbm, a_hbm, x_hbm)

    def loads(kind, img):
        slot = img % 2
        local = pltpu.make_async_copy(sources[kind].at[core * num + img], nat_own.at[kind, slot], load_sem.at[kind, slot])
        push = remote(sources[kind].at[(1 - core) * num + img], nat_rem.at[kind, slot], push_send.at[kind, slot], push_recv.at[kind, slot], partner)
        return local, push

    def start_loads(kind, img):
        for copy in loads(kind, img):
            copy.start()

    def wait_loads(kind, img):
        for copy in loads(kind, img):
            copy.wait()

    def exchange(own, own_slot, oth, oth_slot, send, recv, sem_slot):
        return (
            remote(own.at[own_slot, pl.ds(1, rows)], oth.at[oth_slot, pl.ds(1, rows)], send.at[0, sem_slot], recv.at[0, sem_slot], across),
            remote(own.at[own_slot, halo_src], own.at[own_slot, edge_row], send.at[1, sem_slot], recv.at[1, sem_slot], beside),
            remote(own.at[own_slot, halo_src], oth.at[oth_slot, edge_row], send.at[2, sem_slot], recv.at[2, sem_slot], diagonal),
        )

    def g_exchange(img):
        return exchange(g_own, img % 3, g_oth, img % 2, g_send, g_recv, img % 2)

    def z_exchange(img):
        return exchange(z_own, img % 2, z_oth, img % 2, z_send, z_recv, img % 2)

    def out_copies(img):
        slot = img % 2
        local = pltpu.make_async_copy(out_own.at[slot], dx_hbm.at[core * num + img], out_sem.at[slot])
        push = remote(out_rem.at[slot], dx_hbm.at[core * num + img], out_send.at[slot], out_recv.at[img % 4], partner)
        return local, push

    def wait_out(img):
        for copy in out_copies(img):
            copy.wait()

    def dense(kind, slot, r0, count):
        mine = nat_own[kind, slot, pl.ds(r0, count)]
        theirs = nat_rem[kind, slot, pl.ds(r0, count)]
        return jnp.concatenate([mine, theirs], axis=-1)

    zero_row = jnp.zeros((width, lanes), BF16)
    for slot in range(3):
        g_own[slot, edge_row] = zero_row
    for slot in range(2):
        g_oth[slot, edge_row] = zero_row
        z_own[slot, edge_row] = zero_row
        z_oth[slot, edge_row] = zero_row
    for side in range(3):
        for row in (0, 1, rows + 2, rows + 3):
            shifted[side, row] = zero_row
    acc1[...] = jnp.zeros_like(acc1)
    acc2[...] = jnp.zeros_like(acc2)
    db_ref[...] = jnp.zeros_like(db_ref)

    col = lax.broadcasted_iota(jnp.int32, (m_conv, lanes), 0) % width
    at_first = col == 0
    at_last = col == width - 1

    def from_right(v):
        return jnp.where(at_last, 0.0, pltpu.roll(v, m_conv - 1, 0))

    def from_left(v):
        return jnp.where(at_first, 0.0, pltpu.roll(v, 1, 0))

    def prepare(kind, img):
        @pl.loop(0, rows // CONV_ROWS)
        def _(k):
            r0 = k * CONV_ROWS
            v = dense(kind, img % 2, r0, CONV_ROWS)
            flat = v.reshape(m_conv, lanes).astype(F32)
            shifted[1, pl.ds(r0 + 2, CONV_ROWS)] = v
            shifted[0, pl.ds(r0 + 2, CONV_ROWS)] = from_left(flat).astype(BF16).reshape(v.shape)
            shifted[2, pl.ds(r0 + 2, CONV_ROWS)] = from_right(flat).astype(BF16).reshape(v.shape)

    def both(own, oth, r, count):
        shape = (count * width, lanes)
        return [own[pl.ds(r, count)].reshape(shape), oth[pl.ds(r, count)].reshape(shape)]

    def conv(own, oth, r0, w_ref):
        lhs = jnp.concatenate(sum((both(own, oth, r0 + 2 - kh, CONV_ROWS) for kh in range(3)), []), axis=-1)
        out = jnp.dot(lhs, w_ref[...], preferred_element_type=F32)
        return out[:, lanes:2 * lanes] + from_right(out[:, :lanes]) + from_left(out[:, 2 * lanes:])

    def kgrad(own, oth, acc):
        def piece(r, count):
            lhs = jnp.concatenate(both(own, oth, r, count), axis=-1)
            taps = [shifted[kw, pl.ds(r + kh, count)].reshape(count * width, lanes) for kh in range(3) for kw in range(3)]
            rhs = jnp.concatenate(taps, axis=-1)
            acc[...] += lax.dot_general(lhs, rhs, (((0,), (0,)), ((), ())), preferred_element_type=F32)

        @pl.loop(0, rows // GRAD_ROWS)
        def _(k):
            piece(1 + k * GRAD_ROWS, GRAD_ROWS)

        piece(halo_row, 1)

    def first(img):
        own, oth = g_own.at[img % 3], g_oth.at[img % 2]
        out = z_own.at[img % 2]

        @pl.loop(0, rows // CONV_ROWS)
        def _(k):
            r0 = k * CONV_ROWS
            d_act = conv(own, oth, r0, w2_ref)
            live = shifted[1, pl.ds(r0 + 2, CONV_ROWS)].reshape(m_conv, lanes).astype(F32) > 0
            masked = jnp.where(live, d_act, 0.0)
            db_ref[...] += jnp.sum(masked.reshape(m_conv // 8, 8, lanes), axis=0)
            out[pl.ds(1 + r0, CONV_ROWS)] = masked.astype(BF16).reshape(CONV_ROWS, width, lanes)

    def second(img):
        own, oth = z_own.at[img % 2], z_oth.at[img % 2]
        skip = g_own.at[img % 3]
        slot = img % 2

        @pl.loop(0, rows // CONV_ROWS)
        def _(k):
            r0 = k * CONV_ROWS
            d_x = conv(own, oth, r0, w1_ref)
            d_x = d_x + skip[pl.ds(1 + r0, CONV_ROWS)].reshape(m_conv, lanes).astype(F32)
            d_x = d_x.astype(BF16).reshape(CONV_ROWS, width, lanes)
            out_own[slot, pl.ds(r0, CONV_ROWS)] = d_x[..., :half]
            out_rem[slot, pl.ds(r0, CONV_ROWS)] = d_x[..., half:]

    start_loads(0, 0)
    steps = num + 2

    @pl.loop(0, steps)
    def _(step):
        @pl.when(step >= 1)
        def _():
            for rel in range(4):
                pl.semaphore_wait(free_sem.at[rel], 1)

        @pl.when(step + 1 < num)
        def _():
            start_loads(0, step + 1)

        @pl.when(step < num)
        def _():
            start_loads(1, step)
            wait_loads(0, step)
            dst = g_own.at[step % 3]

            @pl.loop(0, rows // CONV_ROWS)
            def _(k):
                dst[pl.ds(1 + k * CONV_ROWS, CONV_ROWS)] = dense(0, step % 2, k * CONV_ROWS, CONV_ROWS)

            for copy in g_exchange(step):
                copy.start()

        @pl.when((step >= 1) & (step <= num))
        def _():
            img = step - 1
            start_loads(2, img)
            wait_loads(1, img)
            prepare(1, img)
            for copy in g_exchange(img):
                copy.wait()
            first(img)
            for copy in z_exchange(img):
                copy.start()
            kgrad(g_own.at[img % 3], g_oth.at[img % 2], acc2)

        @pl.when(step >= 2)
        def _():
            img = step - 2
            wait_loads(2, img)
            prepare(2, img)

            @pl.when(img >= 2)
            def _():
                wait_out(img - 2)

            for copy in z_exchange(img):
                copy.wait()
            second(img)
            for copy in out_copies(img):
                copy.start()
            kgrad(z_own.at[img % 2], z_oth.at[img % 2], acc1)

        @pl.when(step + 1 < steps)
        def _():
            for rel, peer in enumerate(peers):
                pl.semaphore_signal(free_sem.at[rel], inc=1, device_id=peer, device_id_type=MESH)

    wait_out(num - 2)
    wait_out(num - 1)


def solution(mesh):
    def local_step(x_in, act_saved, w_one, w_two, d_out):
        images, rows, width, half = x_in.shape
        num = images // 2
        lanes = 2 * half
        tp = lax.axis_index("tp")
        swap_cores = [(t, t ^ 1) for t in range(4)]
        swap_rows = [(0, 1), (1, 0)]

        kernels = jnp.stack([w_one, w_two])
        kernels = jnp.concatenate([kernels, lax.ppermute(kernels, "tp", swap_cores)], axis=3)

        def reorder(arr, axis):
            pieces = [lax.dynamic_slice_in_dim(arr, jnp.bitwise_xor(tp, b) * half, half, axis) for b in range(4)]
            return jnp.concatenate(pieces, axis=axis)

        kernels = reorder(kernels, 4).transpose(0, 1, 4, 2, 3).reshape(2, 3 * 4 * half, 3 * lanes)
        pad = (rows + 2, width, lanes)
        dma = pltpu.SemaphoreType.DMA
        hbm = pl.BlockSpec(memory_space=pltpu.HBM)
        vmem = pl.BlockSpec(memory_space=pltpu.VMEM)
        d_x, acc1, acc2, bias = pl.pallas_call(
            lambda *refs: body(num, rows, width, *refs),
            out_shape=(
                jax.ShapeDtypeStruct(x_in.shape, BF16),
                jax.ShapeDtypeStruct((4 * half, TAPS * lanes), F32),
                jax.ShapeDtypeStruct((4 * half, TAPS * lanes), F32),
                jax.ShapeDtypeStruct((8, lanes), F32),
            ),
            in_specs=[hbm, hbm, hbm, vmem, vmem],
            out_specs=[hbm, vmem, vmem, vmem],
            scratch_shapes=[
                pltpu.VMEM((3, 2, rows, width, half), BF16),
                pltpu.VMEM((3, 2, rows, width, half), BF16),
                pltpu.VMEM((3,) + pad, BF16),
                pltpu.VMEM((2,) + pad, BF16),
                pltpu.VMEM((2,) + pad, BF16),
                pltpu.VMEM((2,) + pad, BF16),
                pltpu.VMEM((3, rows + 4, width, lanes), BF16),
                pltpu.VMEM((2, rows, width, half), BF16),
                pltpu.VMEM((2, rows, width, half), BF16),
                dma((3, 2)), dma((3, 2)), dma((3, 2)),
                dma((3, 2)), dma((3, 2)), dma((3, 2)), dma((3, 2)),
                dma((2,)), dma((2,)), dma((4,)),
                pltpu.SemaphoreType.REGULAR((4,)),
            ],
            compiler_params=pltpu.CompilerParams(collective_id=0, has_side_effects=True, vmem_limit_bytes=60 * 1024 * 1024),
        )(x_in, act_saved, d_out, kernels[0], kernels[1])

        sums = jnp.stack([acc1, acc2]).reshape(2, 4 * half, TAPS, lanes)
        sums = reorder(sums, 1)
        bias = jnp.sum(bias, axis=0)
        mine, theirs = sums[..., :half], sums[..., half:]
        mine = mine + lax.ppermute(theirs, "tp", swap_cores)
        bias = bias[:half] + lax.ppermute(bias[half:], "tp", swap_cores)
        mine = mine.transpose(0, 2, 3, 1)
        mine = mine + lax.ppermute(mine, "sp", swap_rows)
        bias = bias + lax.ppermute(bias, "sp", swap_rows)
        grads = mine.reshape(2, 3, 3, half, 4 * half)
        return d_x, grads[0], grads[1], bias

    act_spec = P("dp", "sp", None, "tp")
    kern_spec = P(None, None, "tp", None)
    grad_spec = P("dp", None, "tp", None)
    return jax.shard_map(local_step, mesh=mesh, in_specs=(act_spec, act_spec, kern_spec, kern_spec, act_spec), out_specs=(act_spec, grad_spec, grad_spec, P(("dp", "tp"))), check_vma=False)
```

time: 2750 us -> 815 us (0.30)
  waiting for transfers between devices: 1400 us -> 30.4 us
  Pallas kernels: 0 us -> 746 us
  local copies, waits for them, and re-layouts: 639 us -> 29.7 us
  matrix products: 567 us -> 0 us
  other arithmetic: 99.2 us -> 5.15 us
    all_gather x2 -> x0, waiting for transfers between devices: 1390 us -> none  [the longest x1 771 us: local_step(): dy_pad = lax.all_gather(with_halo(d_out), 'tp', axis=3, tiled=True)]
    pallas_call x0 -> x1, Pallas kernels: none -> 746 us  [local_step(): pl.pallas_call(lambda *refs: body(num, rows, width, *refs), out_shape=(ja...]
    conv_general_dilated x4 -> x0, matrix products: 567 us -> none  [the longest x2 341 us: conv_rows(): lax.conv_general_dilated(padded, kernel[::-1, ::-1], (1, 1), ((0, 0), (1,...]
    all_gather x2 -> x0, local copies, waits for them, and re-layouts: 439 us -> none  [the longest x1 220 us: local_step(): dy_pad = lax.all_gather(with_halo(d_out), 'tp', axis=3, tiled=True)]
    concatenate x1 -> x0, local copies, waits for them, and re-layouts: 66.4 us -> none  [with_halo(): return jnp.concatenate([above, tile, below], axis=1)]
    concatenate x2, other arithmetic: 67.3 us -> 1.06 us  [the longest x1 0.98 us: reorder(): return jnp.concatenate(pieces, axis=axis)]
    unnamed x10 -> x9, local copies, waits for them, and re-layouts: 83.8 us -> 23 us
    ppermute x2 -> x0, local copies, waits for them, and re-layouts: 45.5 us -> none  [the longest x1 23.1 us: with_halo(): above = lax.ppermute(tile[:, -1:], 'sp', to_next)]
  transfers between devices with their start and end apart: 7 -> 5, of which waited for: 4 -> 4; matrix products, arithmetic and copies ran while one was open for 15% -> 0% of each run, Pallas kernels for 0% -> 0%
where the time goes in v1:
time: 815 us
  Pallas kernels  746 us (92%)
  waiting for transfers between devices  30.4 us (4%)
  local copies, waits for them, and re-layouts  29.7 us (4%)
    pallas_call x1, Pallas kernels, local_step(): pl.pallas_call(lambda *refs: body(num, rows, width, *refs), out_shape=(ja...  746 us
    ppermute x1, waiting for transfers between devices, local_step(): bias = bias + lax.ppermute(bias, 'sp', swap_rows)  24.8 us
    unnamed x9, local copies, waits for them, and re-layouts  23 us
  transfers between devices with their start and end apart: 5, of which 4 were waited for; matrix products, arithmetic and copies ran while one was open for 0% of the time, Pallas kernels for 0%

profile of v1, /device:TPU:0, one launch (start us, length us, event | category | flops | bytes accessed | tf_op | source)
XLA Modules:
  0.0 814.7 jit_solution(16192990217113933921)
XLA Ops:
  0.6 0.0 copy-start.1
  0.6 0.0 copy-start
  0.7 1.2 pad_maximum_fusion.2
  1.8 0.9 collective-permute-start
  2.7 1.6 collective-permute-done
  4.3 0.0 copy-done.1
  4.3 0.0 copy-done
  4.3 0.1 pad_maximum_fusion.1
  4.4 0.8 constant_dynamic-slice_fusion.3
  5.2 0.8 maximum_bitcast_fusion
  6.0 0.1 fusion.6
  6.1 0.6 copy.14
  6.8 0.6 copy.13
  7.4 1.2 copy_bitcast_fusion
  8.6 745.8 %shard_map.84 = (bf16[64,64,32,64]{3,2,1,0:T(8,128)(2,1)}, f32[256,1152]{1,0:T(8,128)}, f32[256,1152]{1,0:T(8,128)}, f32[8,128]{1,0:T(8,128)}) custom-call(bf16[64,64,32,64]{3,2,1,0:T(8,128)(2,1)} %refs_0_.1, bf16[64,64,32,64]{3,2,1,0:T(8,128)(2,1)} %refs_1_.1, bf16[64,64,32,64]{3,2,1,0:T(8,128)(2,1)} %refs_2_.1, ...), custom_call_target="tpu_custom_call" | custom-call | tf_op jit(solution)/shard_map/pallas_call | solution.py:255
  754.4 0.0 copy-start.2
  754.4 1.7 copy.15
  756.2 0.0 copy-done.2
  756.2 0.4 copy.16
  756.5 1.3 fusion.1
  757.8 1.0 pad_maximum_fusion
  758.8 0.1 slice.39
  758.9 0.0 copy-start.3
  758.9 0.0 collective-permute-start.1
  759.0 2.8 collective-permute-done.1
  761.8 0.2 fusion.4
  761.9 1.5 collective-permute-start.2
  763.5 0.0 copy-done.3
  763.5 0.1 slice.35
  763.6 0.0 collective-permute-start.3
  763.6 1.2 collective-permute-done.3
  764.7 0.5 collective-permute-start.4
  765.3 24.8 %collective-permute-done.4 = f32[64]{0:T(128)S(1)} collective-permute-done((f32[64]{0:T(128)S(1)}, f32[64]{0:T(128)S(1)}, u32[]{:S(2)}, u32[]{:S(2)}) %collective-permute-start.4) | collective-permute-done | bytes 288 | tf_op jit(solution)/shard_map/ppermute | solution.py:291
  790.0 0.5 add.35
  790.5 0.0 collective-permute-done.2
  790.5 0.2 add.33
  790.7 1.1 fusion.5
  791.8 22.9 %copy.22 = bf16[64,64,32,64]{3,2,1,0:T(8,128)(2,1)} copy(bf16[64,64,32,64]{3,2,1,0:T(8,128)(2,1)} %get-tuple-element.30) | data formatting | bytes 33554432
  (2 shorter events, 0.0 us)
Async XLA Ops:
  0.6 3.7 copy-start.1
  0.6 3.7 copy-start
  1.8 2.5 collective-permute-start
  754.4 1.7 copy-start.2
  758.9 4.6 copy-start.3
  758.9 2.9 collective-permute-start.1
  761.9 28.6 %collective-permute-start.2 = (f32[2,9,64,256]{3,2,1,0:T(8,128)S(1)}, f32[2,9,64,256]{3,2,1,0:T(8,128)S(1)}, u32[]{:S(2)}, u32[]{:S(2)}) collective-permute-start(f32[2,9,64,256]{3,2,1,0:T(8,128)S(1)} %fusion.4), channel_id=1, source_target_pairs={{0,4},{4,0},{1,5},{5,1},{2,6},{6,2},{3,7},{7,3}} | collective-permute-start | bytes 3538952 | tf_op jit(solution)/shard_map/ppermute | solution.py:290
  763.6 1.2 collective-permute-start.3
  764.7 25.3 %collective-permute-start.4 = (f32[64]{0:T(128)S(1)}, f32[64]{0:T(128)S(1)}, u32[]{:S(2)}, u32[]{:S(2)}) collective-permute-start(f32[64]{0:T(128)S(1)} %slice_add_fusion.1), channel_id=1, source_target_pairs={{0,4},{4,0},{1,5},{5,1},{2,6},{6,2},{3,7},{7,3}} | collective-permute-start | bytes 776 | tf_op jit(solution)/shard_map/ppermute | solution.py:291

commit v2 on v1

--- a/solution.py
+++ b/solution.py
@@ -20,8 +20,7 @@
     partner = (dp, sp, tp + 1 - 2 * core)
     across = (dp, sp, (tp + 2) % 4)
     beside = (dp, 1 - sp, tp)
-    diagonal = (dp, 1 - sp, (tp + 2) % 4)
-    peers = (partner, across, beside, diagonal)
+    peers = (partner, across, beside)
     half = 64
     lanes = 2 * half
     edge_row = (rows + 1) * sp
@@ -33,7 +32,7 @@
     barrier = pltpu.get_barrier_semaphore()
     for peer in peers:
         pl.semaphore_signal(barrier, inc=1, device_id=peer, device_id_type=MESH)
-    pl.semaphore_wait(barrier, 4)
+    pl.semaphore_wait(barrier, 3)
 
     def remote(src, dst, send, recv, peer):
         return pltpu.make_async_remote_copy(src_ref=src, dst_ref=dst, send_sem=send, recv_sem=recv, device_id=peer, device_id_type=MESH)
@@ -58,7 +57,7 @@
         return (
             remote(own.at[own_slot, pl.ds(1, rows)], oth.at[oth_slot, pl.ds(1, rows)], send.at[0, sem_slot], recv.at[0, sem_slot], across),
             remote(own.at[own_slot, halo_src], own.at[own_slot, edge_row], send.at[1, sem_slot], recv.at[1, sem_slot], beside),
-            remote(own.at[own_slot, halo_src], oth.at[oth_slot, edge_row], send.at[2, sem_slot], recv.at[2, sem_slot], diagonal),
+            remote(oth.at[oth_slot, halo_src], oth.at[oth_slot, edge_row], send.at[2, sem_slot], recv.at[2, sem_slot], beside),
         )
 
     def g_exchange(img):
@@ -67,15 +66,24 @@
     def z_exchange(img):
         return exchange(z_own, img % 2, z_oth, img % 2, z_send, z_recv, img % 2)
 
-    def out_copies(img):
+    def swap_out(img):
         slot = img % 2
-        local = pltpu.make_async_copy(out_own.at[slot], dx_hbm.at[core * num + img], out_sem.at[slot])
-        push = remote(out_rem.at[slot], dx_hbm.at[core * num + img], out_send.at[slot], out_recv.at[img % 4], partner)
-        return local, push
-
-    def wait_out(img):
-        for copy in out_copies(img):
-            copy.wait()
+        return remote(out_own.at[slot], out_rem.at[slot], out_send.at[slot], out_recv.at[slot], partner)
+
+    def store_out(img):
+        return pltpu.make_async_copy(out_own.at[img % 2], dx_hbm.at[img], out_sem.at[img % 2])
+
+    def finish_out(img):
+        slot = img % 2
+        swap_out(img).wait()
+
+        @pl.loop(0, rows // CONV_ROWS)
+        def _(k):
+            block = pl.ds(k * CONV_ROWS, CONV_ROWS)
+            lane = lax.broadcasted_iota(jnp.int32, (CONV_ROWS, width, lanes), 2)
+            out_own[slot, block] = jnp.where(lane < half, out_own[slot, block], out_rem[slot, block])
+
+        store_out(img).start()
 
     def dense(kind, slot, r0, count):
         mine = nat_own[kind, slot, pl.ds(r0, count)]
@@ -138,32 +146,48 @@
 
         piece(halo_row, 1)
 
-    def first(img):
+    last_block = rows // CONV_ROWS - 1
+
+    def blocks(halo, step):
+        @pl.loop(0, last_block + 1)
+        def _(k):
+            @pl.when(k == last_block)
+            def _():
+                halo.wait()
+
+            step((k + (last_block - 2 * k) * sp) * CONV_ROWS)
+
+    def first(img, halo):
         own, oth = g_own.at[img % 3], g_oth.at[img % 2]
         out = z_own.at[img % 2]
 
-        @pl.loop(0, rows // CONV_ROWS)
-        def _(k):
-            r0 = k * CONV_ROWS
+        def step(r0):
             d_act = conv(own, oth, r0, w2_ref)
             live = shifted[1, pl.ds(r0 + 2, CONV_ROWS)].reshape(m_conv, lanes).astype(F32) > 0
             masked = jnp.where(live, d_act, 0.0)
             db_ref[...] += jnp.sum(masked.reshape(m_conv // 8, 8, lanes), axis=0)
             out[pl.ds(1 + r0, CONV_ROWS)] = masked.astype(BF16).reshape(CONV_ROWS, width, lanes)
 
-    def second(img):
+        blocks(halo, step)
+
+    def second(img, halo):
         own, oth = z_own.at[img % 2], z_oth.at[img % 2]
         skip = g_own.at[img % 3]
         slot = img % 2
 
-        @pl.loop(0, rows // CONV_ROWS)
-        def _(k):
-            r0 = k * CONV_ROWS
+        def step(r0):
             d_x = conv(own, oth, r0, w1_ref)
             d_x = d_x + skip[pl.ds(1 + r0, CONV_ROWS)].reshape(m_conv, lanes).astype(F32)
-            d_x = d_x.astype(BF16).reshape(CONV_ROWS, width, lanes)
-            out_own[slot, pl.ds(r0, CONV_ROWS)] = d_x[..., :half]
-            out_rem[slot, pl.ds(r0, CONV_ROWS)] = d_x[..., half:]
+            out_own[slot, pl.ds(r0, CONV_ROWS)] = d_x.astype(BF16).reshape(CONV_ROWS, width, lanes)
+
+        blocks(halo, step)
+
+    def arrive(copies):
+        main, side, forward = copies
+        main.wait()
+        forward.start()
+        side.wait()
+        return forward
 
     start_loads(0, 0)
     steps = num + 2
@@ -172,7 +196,7 @@
     def _(step):
         @pl.when(step >= 1)
         def _():
-            for rel in range(4):
+            for rel in range(3):
                 pl.semaphore_wait(free_sem.at[rel], 1)
 
         @pl.when(step + 1 < num)
@@ -189,7 +213,7 @@
             def _(k):
                 dst[pl.ds(1 + k * CONV_ROWS, CONV_ROWS)] = dense(0, step % 2, k * CONV_ROWS, CONV_ROWS)
 
-            for copy in g_exchange(step):
+            for copy in g_exchange(step)[:2]:
                 copy.start()
 
         @pl.when((step >= 1) & (step <= num))
@@ -198,10 +222,8 @@
             start_loads(2, img)
             wait_loads(1, img)
             prepare(1, img)
-            for copy in g_exchange(img):
-                copy.wait()
-            first(img)
-            for copy in z_exchange(img):
+            first(img, arrive(g_exchange(img)))
+            for copy in z_exchange(img)[:2]:
                 copy.start()
             kgrad(g_own.at[img % 3], g_oth.at[img % 2], acc2)
 
@@ -211,15 +233,16 @@
             wait_loads(2, img)
             prepare(2, img)
 
+            @pl.when(img >= 1)
+            def _():
+                finish_out(img - 1)
+
             @pl.when(img >= 2)
             def _():
-                wait_out(img - 2)
-
-            for copy in z_exchange(img):
-                copy.wait()
-            second(img)
-            for copy in out_copies(img):
-                copy.start()
+                store_out(img - 2).wait()
+
+            second(img, arrive(z_exchange(img)))
+            swap_out(img).start()
             kgrad(z_own.at[img % 2], z_oth.at[img % 2], acc1)
 
         @pl.when(step + 1 < steps)
@@ -227,8 +250,16 @@
             for rel, peer in enumerate(peers):
                 pl.semaphore_signal(free_sem.at[rel], inc=1, device_id=peer, device_id_type=MESH)
 
-    wait_out(num - 2)
-    wait_out(num - 1)
+    finish_out(num - 1)
+    store_out(num - 2).wait()
+    store_out(num - 1).wait()
+
+
+def unpack(packed, out):
+    core = lax.axis_index("tp") % 2
+    half = out.shape[-1]
+    out[core] = packed[..., :half]
+    out[1 - core] = packed[..., half:]
 
 
 def solution(mesh):
@@ -252,10 +283,10 @@
         dma = pltpu.SemaphoreType.DMA
         hbm = pl.BlockSpec(memory_space=pltpu.HBM)
         vmem = pl.BlockSpec(memory_space=pltpu.VMEM)
-        d_x, acc1, acc2, bias = pl.pallas_call(
+        packed, acc1, acc2, bias = pl.pallas_call(
             lambda *refs: body(num, rows, width, *refs),
             out_shape=(
-                jax.ShapeDtypeStruct(x_in.shape, BF16),
+                jax.ShapeDtypeStruct((num, rows, width, lanes), BF16),
                 jax.ShapeDtypeStruct((4 * half, TAPS * lanes), F32),
                 jax.ShapeDtypeStruct((4 * half, TAPS * lanes), F32),
                 jax.ShapeDtypeStruct((8, lanes), F32),
@@ -270,15 +301,25 @@
                 pltpu.VMEM((2,) + pad, BF16),
                 pltpu.VMEM((2,) + pad, BF16),
                 pltpu.VMEM((3, rows + 4, width, lanes), BF16),
-                pltpu.VMEM((2, rows, width, half), BF16),
-                pltpu.VMEM((2, rows, width, half), BF16),
+                pltpu.VMEM((2, rows, width, lanes), BF16),
+                pltpu.VMEM((2, rows, width, lanes), BF16),
                 dma((3, 2)), dma((3, 2)), dma((3, 2)),
                 dma((3, 2)), dma((3, 2)), dma((3, 2)), dma((3, 2)),
-                dma((2,)), dma((2,)), dma((4,)),
-                pltpu.SemaphoreType.REGULAR((4,)),
+                dma((2,)), dma((2,)), dma((2,)),
+                pltpu.SemaphoreType.REGULAR((3,)),
             ],
             compiler_params=pltpu.CompilerParams(collective_id=0, has_side_effects=True, vmem_limit_bytes=60 * 1024 * 1024),
         )(x_in, act_saved, d_out, kernels[0], kernels[1])
+
+        group = 2
+        d_x = pl.pallas_call(
+            unpack,
+            grid=(num // group,),
+            out_shape=jax.ShapeDtypeStruct((2, num, rows, width, half), BF16),
+            in_specs=[pl.BlockSpec((group, rows, width, lanes), lambda i: (i, 0, 0, 0))],
+            out_specs=pl.BlockSpec((2, group, rows, width, half), lambda i: (0, i, 0, 0, 0)),
+            cost_estimate=pl.CostEstimate(flops=10**10, bytes_accessed=5 * 10**7, transcendentals=0),
+        )(packed).reshape(x_in.shape)
 
         sums = jnp.stack([acc1, acc2]).reshape(2, 4 * half, TAPS, lanes)
         sums = reorder(sums, 1)

time: 815 us -> 782 us (0.960)
  local copies, waits for them, and re-layouts: 29.7 us -> 6.72 us
  waiting for transfers between devices: 30.4 us -> 7.46 us
  Pallas kernels: 746 us -> 759 us
    unnamed x9 -> x8, local copies, waits for them, and re-layouts: 23 us -> 0.02 us
    ppermute x1, waiting for transfers between devices: 24.8 us -> 1.84 us  [local_step(): bias = bias + lax.ppermute(bias, 'sp', swap_rows)]
    pallas_call x0 -> x1, Pallas kernels: none -> 22.9 us  [local_step(): pl.pallas_call(unpack, grid=(num // group,), out_shape=jax.ShapeDtypeStru...]
    pallas_call x1, Pallas kernels: 746 us -> 736 us  [local_step(): pl.pallas_call(lambda *refs: body(num, rows, width, *refs), out_shape=(ja...]
  transfers between devices with their start and end apart: 5 -> 5, of which waited for: 4 -> 4; matrix products, arithmetic and copies ran while one was open for 0% -> 0% of each run, Pallas kernels for 0% -> 3%
where the time goes in v2:
time: 782 us
  Pallas kernels  759 us (97%)
    pallas_call x1, Pallas kernels, local_step(): pl.pallas_call(lambda *refs: body(num, rows, width, *refs), out_shape=(ja...  736 us
    pallas_call x1, Pallas kernels, local_step(): pl.pallas_call(unpack, grid=(num // group,), out_shape=jax.ShapeDtypeStru...  22.9 us
  transfers between devices with their start and end apart: 5, of which 4 were waited for; matrix products, arithmetic and copies ran while one was open for 0% of the time, Pallas kernels for 3%

profile of v2, /device:TPU:0, one launch (start us, length us, event | category | flops | bytes accessed | tf_op | source)
XLA Modules:
  0.0 781.7 jit_solution(3731113363176966243)
XLA Ops:
  0.6 0.0 copy-start
  0.6 0.0 copy-start.1
  0.7 1.2 pad_maximum_fusion.2
  1.8 0.9 collective-permute-start
  2.7 1.6 collective-permute-done
  4.3 0.0 copy-done
  4.3 0.0 copy-done.1
  4.3 0.1 pad_maximum_fusion.1
  4.4 0.8 constant_dynamic-slice_fusion.3
  5.2 0.8 maximum_bitcast_fusion
  6.0 0.1 fusion.6
  6.1 0.6 copy.14
  6.8 0.6 copy.13
  7.4 1.2 copy_bitcast_fusion
  8.6 735.7 %shard_map.84 = (bf16[32,64,32,128]{3,2,1,0:T(8,128)(2,1)}, f32[256,1152]{1,0:T(8,128)}, f32[256,1152]{1,0:T(8,128)}, f32[8,128]{1,0:T(8,128)}) custom-call(bf16[64,64,32,64]{3,2,1,0:T(8,128)(2,1)} %refs_0_.1, bf16[64,64,32,64]{3,2,1,0:T(8,128)(2,1)} %refs_1_.1, bf16[64,64,32,64]{3,2,1,0:T(8,128)(2,1)} %refs_2_.1, ...), custom_call_target="tpu_custom_call" | custom-call | tf_op jit(solution)/shard_map/pallas_call | solution.py:286
  744.3 0.0 copy-start.2
  744.3 1.7 copy.15
  746.0 0.0 copy-done.2
  746.1 0.4 copy.16
  746.4 1.3 fusion.1
  747.7 1.0 pad_maximum_fusion
  748.7 0.1 slice.39
  748.8 0.0 copy-start.3
  748.8 0.0 collective-permute-start.1
  748.8 2.8 collective-permute-done.1
  751.7 0.2 fusion.4
  751.8 1.5 collective-permute-start.2
  753.3 0.0 copy-done.3
  753.4 0.1 slice.35
  753.4 0.0 collective-permute-start.3
  753.4 1.2 collective-permute-done.3
  754.6 0.5 collective-permute-start.4
  755.1 22.9 %shard_map.85 = bf16[2,32,64,32,64]{4,3,2,1,0:T(8,128)(2,1)} custom-call(bf16[32,64,32,128]{3,2,1,0:T(8,128)(2,1)} %get-tuple-element.8.packed), custom_call_target="tpu_custom_call" | custom-call | flops 10000000000 | bytes 50000000 | tf_op jit(solution)/shard_map/pallas_call | solution.py:315
  778.1 1.8 collective-permute-done.4
  779.9 0.5 add.35
  780.4 0.0 collective-permute-done.2
  780.4 0.2 add.33
  780.6 1.1 fusion.5
  (2 shorter events, 0.0 us)
Async XLA Ops:
  0.6 3.7 copy-start
  0.6 3.7 copy-start.1
  1.8 2.5 collective-permute-start
  744.3 1.7 copy-start.2
  748.8 4.6 copy-start.3
  748.8 2.9 collective-permute-start.1
  751.8 28.6 %collective-permute-start.2 = (f32[2,9,64,256]{3,2,1,0:T(8,128)S(1)}, f32[2,9,64,256]{3,2,1,0:T(8,128)S(1)}, u32[]{:S(2)}, u32[]{:S(2)}) collective-permute-start(f32[2,9,64,256]{3,2,1,0:T(8,128)S(1)} %fusion.4), channel_id=1, source_target_pairs={{0,4},{4,0},{1,5},{5,1},{2,6},{6,2},{3,7},{7,3}} | collective-permute-start | bytes 3538952 | tf_op jit(solution)/shard_map/ppermute | solution.py:331
  753.4 1.2 collective-permute-start.3
  754.6 25.3 %collective-permute-start.4 = (f32[64]{0:T(128)S(1)}, f32[64]{0:T(128)S(1)}, u32[]{:S(2)}, u32[]{:S(2)}) collective-permute-start(f32[64]{0:T(128)S(1)} %slice_add_fusion.1), channel_id=1, source_target_pairs={{0,4},{4,0},{1,5},{5,1},{2,6},{6,2},{3,7},{7,3}} | collective-permute-start | bytes 776 | tf_op jit(solution)/shard_map/ppermute | solution.py:332

commit v3 on v2

v3 whole, which is shorter than its diff:
```python
import jax
import jax.numpy as jnp
from jax import lax
from jax.experimental import pallas as pl
from jax.experimental.pallas import tpu as pltpu
from jax.sharding import PartitionSpec as P

MESH = pl.DeviceIdType.MESH
F32, BF16 = jnp.float32, jnp.bfloat16
TAPS = 9
CONV_ROWS = 16
GRAD_ROWS = 32


def body(num, rows, width, x_hbm, a_hbm, y_hbm, w1_hbm, w2_hbm, dx_hbm, dw1_ref, dw2_ref,
         acc1, acc2, db_ref, raw_own, raw_rem, weights, part_own, part_send, part_recv, row_recv, nat_own, nat_rem, g_own, g_oth, z_own, z_oth, shifted, out_own, out_rem,
         load_sem, push_send, push_recv, g_send, g_recv, z_send, z_recv, out_sem, out_send, out_recv, raw_sem, raw_send, raw_recv, part_sems, free_sem):
    dp, sp, tp = lax.axis_index("dp"), lax.axis_index("sp"), lax.axis_index("tp")
    core, chip = tp % 2, tp // 2
    partner = (dp, sp, tp + 1 - 2 * core)
    across = (dp, sp, (tp + 2) % 4)
    beside = (dp, 1 - sp, tp)
    peers = (partner, across, beside)
    half = 64
    lanes = 2 * half
    edge_row = (rows + 1) * sp
    halo_row = (rows + 1) * (1 - sp)
    halo_src = rows - (rows - 1) * sp
    m_conv = CONV_ROWS * width
    m_grad = GRAD_ROWS * width

    barrier = pltpu.get_barrier_semaphore()
    for peer in peers:
        pl.semaphore_signal(barrier, inc=1, device_id=peer, device_id_type=MESH)
    pl.semaphore_wait(barrier, 3)

    def remote(src, dst, send, recv, peer):
        return pltpu.make_async_remote_copy(src_ref=src, dst_ref=dst, send_sem=send, recv_sem=recv, device_id=peer, device_id_type=MESH)

    sources = (y_hbm, a_hbm, x_hbm)

    def loads(kind, img):
        slot = img % 2
        local = pltpu.make_async_copy(sources[kind].at[core * num + img], nat_own.at[kind, slot], load_sem.at[kind, slot])
        push = remote(sources[kind].at[(1 - core) * num + img], nat_rem.at[kind, slot], push_send.at[kind, slot], push_recv.at[kind, slot], partner)
        return local, push

    def start_loads(kind, img):
        for copy in loads(kind, img):
            copy.start()

    def wait_loads(kind, img):
        for copy in loads(kind, img):
            copy.wait()

    def exchange(own, own_slot, oth, oth_slot, send, recv, sem_slot):
        return (
            remote(own.at[own_slot, pl.ds(1, rows)], oth.at[oth_slot, pl.ds(1, rows)], send.at[0, sem_slot], recv.at[0, sem_slot], across),
            remote(own.at[own_slot, halo_src], own.at[own_slot, edge_row], send.at[1, sem_slot], recv.at[1, sem_slot], beside),
            remote(oth.at[oth_slot, halo_src], oth.at[oth_slot, edge_row], send.at[2, sem_slot], recv.at[2, sem_slot], beside),
        )

    def g_exchange(img):
        return exchange(g_own, img % 3, g_oth, img % 2, g_send, g_recv, img % 2)

    def z_exchange(img):
        return exchange(z_own, img % 2, z_oth, img % 2, z_send, z_recv, img % 2)

    def swap_out(img):
        slot = img % 2
        return remote(out_own.at[slot], out_rem.at[slot], out_send.at[slot], out_recv.at[slot], partner)

    def store_out(img):
        return pltpu.make_async_copy(out_own.at[img % 2], dx_hbm.at[img], out_sem.at[img % 2])

    def finish_out(img):
        slot = img % 2
        swap_out(img).wait()

        @pl.loop(0, rows // CONV_ROWS)
        def _(k):
            block = pl.ds(k * CONV_ROWS, CONV_ROWS)
            lane = lax.broadcasted_iota(jnp.int32, (CONV_ROWS, width, lanes), 2)
            out_own[slot, block] = jnp.where(lane < half, out_own[slot, block], out_rem[slot, block])

        store_out(img).start()

    def dense(kind, slot, r0, count):
        mine = nat_own[kind, slot, pl.ds(r0, count)]
        theirs = nat_rem[kind, slot, pl.ds(r0, count)]
        return jnp.concatenate([mine, theirs], axis=-1)

    col = lax.broadcasted_iota(jnp.int32, (m_conv, lanes), 0) % width
    at_first = col == 0
    at_last = col == width - 1

    def from_right(v):
        return jnp.where(at_last, 0.0, pltpu.roll(v, m_conv - 1, 0))

    def from_left(v):
        return jnp.where(at_first, 0.0, pltpu.roll(v, 1, 0))

    def prepare(kind, img):
        @pl.loop(0, rows // CONV_ROWS)
        def _(k):
            r0 = k * CONV_ROWS
            v = dense(kind, img % 2, r0, CONV_ROWS)
            flat = v.reshape(m_conv, lanes).astype(F32)
            shifted[1, pl.ds(r0 + 2, CONV_ROWS)] = v
            shifted[0, pl.ds(r0 + 2, CONV_ROWS)] = from_left(flat).astype(BF16).reshape(v.shape)
            shifted[2, pl.ds(r0 + 2, CONV_ROWS)] = from_right(flat).astype(BF16).reshape(v.shape)

    def both(own, oth, r, count):
        shape = (count * width, lanes)
        return [own[pl.ds(r, count)].reshape(shape), oth[pl.ds(r, count)].reshape(shape)]

    def conv(own, oth, r0, w_ref):
        lhs = jnp.concatenate(sum((both(own, oth, r0 + 2 - kh, CONV_ROWS) for kh in range(3)), []), axis=-1)
        out = jnp.dot(lhs, w_ref[...], preferred_element_type=F32)
        return out[:, lanes:2 * lanes] + from_right(out[:, :lanes]) + from_left(out[:, 2 * lanes:])

    def kgrad(own, oth, acc):
        def piece(r, count):
            lhs = jnp.concatenate(both(own, oth, r, count), axis=-1)
            taps = [shifted[kw, pl.ds(r + kh, count)].reshape(count * width, lanes) for kh in range(3) for kw in range(3)]
            rhs = jnp.concatenate(taps, axis=-1)
            acc[...] += lax.dot_general(lhs, rhs, (((0,), (0,)), ((), ())), preferred_element_type=F32)

        @pl.loop(0, rows // GRAD_ROWS)
        def _(k):
            piece(1 + k * GRAD_ROWS, GRAD_ROWS)

        piece(halo_row, 1)

    last_block = rows // CONV_ROWS - 1

    def blocks(halo, step):
        @pl.loop(0, last_block + 1)
        def _(k):
            @pl.when(k == last_block)
            def _():
                halo.wait()

            step((k + (last_block - 2 * k) * sp) * CONV_ROWS)

    def first(img, halo):
        own, oth = g_own.at[img % 3], g_oth.at[img % 2]
        out = z_own.at[img % 2]

        def step(r0):
            d_act = conv(own, oth, r0, weights.at[1])
            live = shifted[1, pl.ds(r0 + 2, CONV_ROWS)].reshape(m_conv, lanes).astype(F32) > 0
            masked = jnp.where(live, d_act, 0.0)
            db_ref[...] += jnp.sum(masked.reshape(m_conv // 8, 8, lanes), axis=0)
            out[pl.ds(1 + r0, CONV_ROWS)] = masked.astype(BF16).reshape(CONV_ROWS, width, lanes)

        blocks(halo, step)

    def second(img, halo):
        own, oth = z_own.at[img % 2], z_oth.at[img % 2]
        skip = g_own.at[img % 3]
        slot = img % 2

        def step(r0):
            d_x = conv(own, oth, r0, weights.at[0])
            d_x = d_x + skip[pl.ds(1 + r0, CONV_ROWS)].reshape(m_conv, lanes).astype(F32)
            out_own[slot, pl.ds(r0, CONV_ROWS)] = d_x.astype(BF16).reshape(CONV_ROWS, width, lanes)

        blocks(halo, step)

    def arrive(copies):
        main, side, forward = copies
        main.wait()
        forward.start()
        side.wait()
        return forward

    def raw_copies():
        copies = []
        for idx, src in enumerate((w1_hbm, w2_hbm)):
            copies.append(pltpu.make_async_copy(src, raw_own.at[idx], raw_sem.at[idx]))
            copies.append(remote(src, raw_rem.at[idx], raw_send.at[idx], raw_recv.at[idx], partner))
        return copies

    def local_block(block):
        on_chip = chip if block < 2 else 1 - chip
        on_core = core if block % 2 == 0 else 1 - core
        return pl.multiple_of((2 * on_chip + on_core) * half, half)

    def build_weights():
        for copy in raw_copies():
            copy.wait()
        for idx in range(2):
            @pl.loop(0, 3)
            def _(kh):
                for kw in range(3):
                    taps = jnp.concatenate([raw_own[idx, kh, kw], raw_rem[idx, kh, kw]], axis=0).T
                    for block in range(4):
                        dst = pl.ds(pl.multiple_of(kh * 4 * half, half) + local_block(block), half)
                        weights[idx, dst, kw * lanes:(kw + 1) * lanes] = taps[block * half:(block + 1) * half]

    grad_rows = TAPS * half

    def collect(acc, idx):
        @pl.loop(0, TAPS)
        def _(tap):
            cols = pl.ds(pl.multiple_of(tap * lanes, lanes), lanes)
            flipped = jnp.concatenate([acc[pl.ds(local_block(block), half), cols] for block in range(4)], axis=0).T
            dst = pl.ds(pl.multiple_of(tap * half, half), half)
            part_own[idx, dst] = flipped[:half]
            part_send[idx, dst] = flipped[half:]

    def swap_part(idx):
        return remote(part_send.at[idx], part_recv.at[idx], part_sems.at[idx, 0], part_sems.at[idx, 1], partner)

    def swap_rows():
        return remote(part_own.at[1], row_recv, part_sems.at[2, 0], part_sems.at[2, 1], beside)

    def add_part(idx):
        swap_part(idx).wait()
        part_own[idx] += part_recv[idx]

    start_loads(0, 0)
    for copy in raw_copies():
        copy.start()
    steps = num + 2
    zero_row = jnp.zeros((width, lanes), BF16)
    for slot in range(3):
        g_own[slot, edge_row] = zero_row
    for slot in range(2):
        g_oth[slot, edge_row] = zero_row
        z_own[slot, edge_row] = zero_row
        z_oth[slot, edge_row] = zero_row
    for side in range(3):
        for row in (0, 1, rows + 2, rows + 3):
            shifted[side, row] = zero_row
    tail = pl.ds(grad_rows, 8)
    for idx in range(2):
        part_own[idx, tail] = jnp.zeros((8, 2 * lanes), F32)
        part_send[idx, tail] = jnp.zeros((8, 2 * lanes), F32)

    @pl.loop(0, steps)
    def _(step):
        @pl.when(step >= 1)
        def _():
            for rel in range(3):
                pl.semaphore_wait(free_sem.at[rel], 1)

        @pl.when(step + 1 < num)
        def _():
            start_loads(0, step + 1)

        @pl.when(step < num)
        def _():
            start_loads(1, step)
            wait_loads(0, step)
            dst = g_own.at[step % 3]

            @pl.loop(0, rows // CONV_ROWS)
            def _(k):
                dst[pl.ds(1 + k * CONV_ROWS, CONV_ROWS)] = dense(0, step % 2, k * CONV_ROWS, CONV_ROWS)

            for copy in g_exchange(step)[:2]:
                copy.start()

        @pl.when(step == 0)
        def _():
            build_weights()
            acc1[...] = jnp.zeros_like(acc1)
            acc2[...] = jnp.zeros_like(acc2)
            db_ref[...] = jnp.zeros_like(db_ref)

        @pl.when((step >= 1) & (step <= num))
        def _():
            img = step - 1
            start_loads(2, img)
            wait_loads(1, img)
            prepare(1, img)
            first(img, arrive(g_exchange(img)))
            for copy in z_exchange(img)[:2]:
                copy.start()
            kgrad(g_own.at[img % 3], g_oth.at[img % 2], acc2)

            @pl.when(img == num - 1)
            def _():
                collect(acc2, 1)
                part_own[1, tail, :lanes] = db_ref[...]
                part_send[1, tail, :lanes] = pltpu.roll(db_ref[...], half, 1)
                swap_part(1).start()

        @pl.when(step >= 2)
        def _():
            img = step - 2
            wait_loads(2, img)
            prepare(2, img)

            @pl.when(img >= 1)
            def _():
                finish_out(img - 1)

            @pl.when(img >= 2)
            def _():
                store_out(img - 2).wait()

            second(img, arrive(z_exchange(img)))
            swap_out(img).start()
            kgrad(z_own.at[img % 2], z_oth.at[img % 2], acc1)

            @pl.when(img == num - 2)
            def _():
                add_part(1)
                swap_rows().start()

        @pl.when(step + 1 < steps)
        def _():
            for rel, peer in enumerate(peers):
                pl.semaphore_signal(free_sem.at[rel], inc=1, device_id=peer, device_id_type=MESH)

    collect(acc1, 0)
    swap_part(0).start()
    finish_out(num - 1)
    swap_rows().wait()
    dw2_ref[...] = part_own[1] + row_recv[...]
    add_part(0)
    dw1_ref[...] = part_own[0, :grad_rows]
    store_out(num - 2).wait()
    store_out(num - 1).wait()


def unpack(num, packed_hbm, out_hbm, packed, out, load_sem, store_sem):
    core = lax.axis_index("tp") % 2
    depth, half = packed.shape[0], out.shape[-1]

    def load(i):
        slot = i % depth
        return pltpu.make_async_copy(packed_hbm.at[i], packed.at[slot], load_sem.at[slot])

    def stores(i):
        slot = i % depth
        return [pltpu.make_async_copy(out.at[slot, side], out_hbm.at[side, i], store_sem.at[slot, side]) for side in range(2)]

    for i in range(depth):
        load(i).start()

    @pl.loop(0, num)
    def _(i):
        slot = i % depth
        load(i).wait()

        @pl.when(i >= depth)
        def _():
            for copy in stores(i - depth):
                copy.wait()

        out[slot, core] = packed[slot, ..., :half]
        out[slot, 1 - core] = packed[slot, ..., half:]
        for copy in stores(i):
            copy.start()

        @pl.when(i + depth < num)
        def _():
            load(i + depth).start()

    for i in range(num - depth, num):
        for copy in stores(i):
            copy.wait()


def solution(mesh):
    def local_step(x_in, act_saved, w_one, w_two, d_out):
        images, rows, width, half = x_in.shape
        num = images // 2
        lanes = 2 * half
        swap_rows = [(0, 1), (1, 0)]
        part = pltpu.VMEM((2, TAPS * half + 8, 4 * half), F32)
        pad = (rows + 2, width, lanes)
        dma = pltpu.SemaphoreType.DMA
        hbm = pl.BlockSpec(memory_space=pltpu.HBM)
        vmem = pl.BlockSpec(memory_space=pltpu.VMEM)
        packed, grad_one, grad_two = pl.pallas_call(
            lambda *refs: body(num, rows, width, *refs),
            out_shape=(
                jax.ShapeDtypeStruct((num, rows, width, lanes), BF16),
                jax.ShapeDtypeStruct((TAPS * half, 4 * half), F32),
                jax.ShapeDtypeStruct((TAPS * half + 8, 4 * half), F32),
            ),
            in_specs=[hbm] * 5,
            out_specs=[hbm, vmem, vmem],
            scratch_shapes=[
                pltpu.VMEM((4 * half, TAPS * lanes), F32),
                pltpu.VMEM((4 * half, TAPS * lanes), F32),
                pltpu.VMEM((8, lanes), F32),
                pltpu.VMEM((2,) + w_one.shape, BF16),
                pltpu.VMEM((2,) + w_one.shape, BF16),
                pltpu.VMEM((2, 3 * 4 * half, 3 * lanes), BF16),
                part, part, part,
                pltpu.VMEM((TAPS * half + 8, 4 * half), F32),
                pltpu.VMEM((3, 2, rows, width, half), BF16),
                pltpu.VMEM((3, 2, rows, width, half), BF16),
                pltpu.VMEM((3,) + pad, BF16),
                pltpu.VMEM((2,) + pad, BF16),
                pltpu.VMEM((2,) + pad, BF16),
                pltpu.VMEM((2,) + pad, BF16),
                pltpu.VMEM((3, rows + 4, width, lanes), BF16),
                pltpu.VMEM((2, rows, width, lanes), BF16),
                pltpu.VMEM((2, rows, width, lanes), BF16),
                dma((3, 2)), dma((3, 2)), dma((3, 2)),
                dma((3, 2)), dma((3, 2)), dma((3, 2)), dma((3, 2)),
                dma((2,)), dma((2,)), dma((2,)),
                dma((2,)), dma((2,)), dma((2,)), dma((3, 2)),
                pltpu.SemaphoreType.REGULAR((3,)),
            ],
            compiler_params=pltpu.CompilerParams(collective_id=0, has_side_effects=True, vmem_limit_bytes=60 * 1024 * 1024),
        )(x_in, act_saved, d_out, w_one, w_two)

        depth = 8
        d_x = pl.pallas_call(
            lambda *refs: unpack(num, *refs),
            out_shape=jax.ShapeDtypeStruct((2, num, rows, width, half), BF16),
            in_specs=[hbm],
            out_specs=hbm,
            scratch_shapes=[
                pltpu.VMEM((depth, rows, width, lanes), BF16),
                pltpu.VMEM((depth, 2, rows, width, half), BF16),
                dma((depth,)), dma((depth, 2)),
            ],
            cost_estimate=pl.CostEstimate(flops=10**10, bytes_accessed=5 * 10**7, transcendentals=0),
        )(packed).reshape(x_in.shape)

        grad_one = grad_one + lax.ppermute(grad_one, "sp", swap_rows)
        bias = jnp.sum(grad_two[TAPS * half:, :half], axis=0)
        grad_two = grad_two[:TAPS * half]
        return d_x, grad_one.reshape(w_one.shape), grad_two.reshape(w_two.shape), bias

    act_spec = P("dp", "sp", None, "tp")
    kern_spec = P(None, None, "tp", None)
    grad_spec = P("dp", None, "tp", None)
    return jax.shard_map(local_step, mesh=mesh, in_specs=(act_spec, act_spec, kern_spec, kern_spec, act_spec), out_specs=(act_spec, grad_spec, grad_spec, P(("dp", "tp"))), check_vma=False)
```

time: 782 us -> 764 us (0.977)
  transfers between devices with their start and end apart: 5 -> 1, of which waited for: 4 -> 0; matrix products, arithmetic and copies ran while one was open for 0% -> 0% of each run, Pallas kernels for 3% -> 2%
where the time goes in v3:
time: 764 us
  Pallas kernels  759 us (99%)
    pallas_call x1, Pallas kernels, local_step(): pl.pallas_call(lambda *refs: body(num, rows, width, *refs), out_shape=(ja...  742 us
    pallas_call x1, Pallas kernels, local_step(): pl.pallas_call(lambda *refs: unpack(num, *refs), out_shape=jax.ShapeDtype...  16.3 us
  transfers between devices with their start and end apart: 1, of which 0 were waited for; matrix products, arithmetic and copies ran while one was open for 0% of the time, Pallas kernels for 2%

profile of v3, /device:TPU:0, one launch (start us, length us, event | category | flops | bytes accessed | tf_op | source)
XLA Modules:
  0.0 764.0 jit_solution(11105347177147562966)
XLA Ops:
  0.6 742.3 %shard_map.84 = (bf16[32,64,32,128]{3,2,1,0:T(8,128)(2,1)}, f32[576,256]{1,0:T(8,128)}, f32[584,256]{1,0:T(8,128)}) custom-call(bf16[64,64,32,64]{3,2,1,0:T(8,128)(2,1)} %refs_0_.1, bf16[64,64,32,64]{3,2,1,0:T(8,128)(2,1)} %refs_1_.1, bf16[64,64,32,64]{3,2,1,0:T(8,128)(2,1)} %refs_2_.1, bf16[3,3,64,256]{3,2,1,0:T(8,128)(2,1)} %refs_3_.1, ...), custom_call_target="tpu_custom_call" | custom-call | tf_op jit(solution)/shard_map/pallas_call | solution.py:380
  742.9 0.0 copy-start
  742.9 0.7 collective-permute-start
  743.7 1.2 slice_reduce_fusion
  744.9 1.9 slice.6
  746.8 16.3 %shard_map.85 = bf16[2,32,64,32,64]{4,3,2,1,0:T(8,128)(2,1)} custom-call(bf16[32,64,32,128]{3,2,1,0:T(8,128)(2,1)} %get-tuple-element.7.refs_0_), custom_call_target="tpu_custom_call" | custom-call | flops 10000000000 | bytes 50000000 | tf_op jit(solution)/shard_map/pallas_call | solution.py:417
  763.1 0.0 collective-permute-done
  763.1 0.0 copy-done
  763.1 0.9 add.3
Async XLA Ops:
  742.9 20.2 %copy-start = (f32[576,256]{1,0:T(8,128)S(1)}, f32[576,256]{1,0:T(8,128)}, u32[]{:S(2)}) copy-start(f32[576,256]{1,0:T(8,128)} %get-tuple-element.8) | copy-start | bytes 1769476
  742.9 20.2 %collective-permute-start = (f32[576,256]{1,0:T(8,128)}, f32[576,256]{1,0:T(8,128)S(1)}, u32[]{:S(2)}, u32[]{:S(2)}) collective-permute-start(f32[576,256]{1,0:T(8,128)} %get-tuple-element.8), channel_id=1, source_target_pairs={{0,4},{4,0},{1,5},{5,1},{2,6},{6,2},{3,7},{7,3}} | collective-permute-start | bytes 1769480 | tf_op jit(solution)/shard_map/ppermute | solution.py:430

commit v4 on v3

--- a/solution.py
+++ b/solution.py
@@ -12,7 +12,7 @@
 GRAD_ROWS = 32
 
 
-def body(num, rows, width, x_hbm, a_hbm, y_hbm, w1_hbm, w2_hbm, dx_hbm, dw1_ref, dw2_ref,
+def body(num, rows, width, x_hbm, a_hbm, y_hbm, w1_hbm, w2_hbm, dx_hbm, dw1_hbm, dw2_hbm,
          acc1, acc2, db_ref, raw_own, raw_rem, weights, part_own, part_send, part_recv, row_recv, nat_own, nat_rem, g_own, g_oth, z_own, z_oth, shifted, out_own, out_rem,
          load_sem, push_send, push_recv, g_send, g_recv, z_send, z_recv, out_sem, out_send, out_recv, raw_sem, raw_send, raw_recv, part_sems, free_sem):
     dp, sp, tp = lax.axis_index("dp"), lax.axis_index("sp"), lax.axis_index("tp")
@@ -126,11 +126,12 @@
             rhs = jnp.concatenate(taps, axis=-1)
             acc[...] += lax.dot_general(lhs, rhs, (((0,), (0,)), ((), ())), preferred_element_type=F32)
 
-        @pl.loop(0, rows // GRAD_ROWS)
-        def _(k):
-            piece(1 + k * GRAD_ROWS, GRAD_ROWS)
-
-        piece(halo_row, 1)
+        def inner():
+            @pl.loop(0, rows // GRAD_ROWS)
+            def _(k):
+                piece(1 + k * GRAD_ROWS, GRAD_ROWS)
+
+        return inner, lambda: piece(halo_row, 1)
 
     last_block = rows // CONV_ROWS - 1
 
@@ -279,7 +280,8 @@
             first(img, arrive(g_exchange(img)))
             for copy in z_exchange(img)[:2]:
                 copy.start()
-            kgrad(g_own.at[img % 3], g_oth.at[img % 2], acc2)
+            for part in kgrad(g_own.at[img % 3], g_oth.at[img % 2], acc2):
+                part()
 
             @pl.when(img == num - 1)
             def _():
@@ -302,15 +304,18 @@
             def _():
                 store_out(img - 2).wait()
 
-            second(img, arrive(z_exchange(img)))
-            swap_out(img).start()
-            kgrad(z_own.at[img % 2], z_oth.at[img % 2], acc1)
-
             @pl.when(img == num - 2)
             def _():
                 add_part(1)
                 swap_rows().start()
 
+            halo = arrive(z_exchange(img))
+            inner, outer = kgrad(z_own.at[img % 2], z_oth.at[img % 2], acc1)
+            inner()
+            second(img, halo)
+            swap_out(img).start()
+            outer()
+
         @pl.when(step + 1 < steps)
         def _():
             for rel, peer in enumerate(peers):
@@ -320,14 +325,19 @@
     swap_part(0).start()
     finish_out(num - 1)
     swap_rows().wait()
-    dw2_ref[...] = part_own[1] + row_recv[...]
+    part_own[1] += row_recv[...]
+    second_grad = pltpu.make_async_copy(part_own.at[1], dw2_hbm, raw_sem.at[1])
+    second_grad.start()
     add_part(0)
-    dw1_ref[...] = part_own[0, :grad_rows]
+    first_grad = pltpu.make_async_copy(part_own.at[0, pl.ds(0, grad_rows)], dw1_hbm, raw_sem.at[0])
+    first_grad.start()
     store_out(num - 2).wait()
     store_out(num - 1).wait()
-
-
-def unpack(num, packed_hbm, out_hbm, packed, out, load_sem, store_sem):
+    second_grad.wait()
+    first_grad.wait()
+
+
+def unpack(num, packed_hbm, grad_hbm, out_hbm, grad_out, bias_out, packed, out, grad, bias, load_sem, store_sem, grad_sem):
     core = lax.axis_index("tp") % 2
     depth, half = packed.shape[0], out.shape[-1]
 
@@ -339,14 +349,25 @@
         slot = i % depth
         return [pltpu.make_async_copy(out.at[slot, side], out_hbm.at[side, i], store_sem.at[slot, side]) for side in range(2)]
 
+    load_grad = pltpu.make_async_copy(grad_hbm, grad, grad_sem.at[0])
+    store_grad = pltpu.make_async_copy(grad.at[pl.ds(0, TAPS * half)], grad_out, grad_sem.at[0])
+    store_bias = pltpu.make_async_copy(bias, bias_out, grad_sem.at[1])
     for i in range(depth):
         load(i).start()
+    load_grad.start()
 
     @pl.loop(0, num)
     def _(i):
         slot = i % depth
         load(i).wait()
 
+        @pl.when(i == depth)
+        def _():
+            load_grad.wait()
+            store_grad.start()
+            bias[...] = jnp.sum(grad[TAPS * half:, :half], axis=0, keepdims=True)
+            store_bias.start()
+
         @pl.when(i >= depth)
         def _():
             for copy in stores(i - depth):
@@ -364,6 +385,8 @@
     for i in range(num - depth, num):
         for copy in stores(i):
             copy.wait()
+    store_grad.wait()
+    store_bias.wait()
 
 
 def solution(mesh):
@@ -376,7 +399,6 @@
         pad = (rows + 2, width, lanes)
         dma = pltpu.SemaphoreType.DMA
         hbm = pl.BlockSpec(memory_space=pltpu.HBM)
-        vmem = pl.BlockSpec(memory_space=pltpu.VMEM)
         packed, grad_one, grad_two = pl.pallas_call(
             lambda *refs: body(num, rows, width, *refs),
             out_shape=(
@@ -385,7 +407,7 @@
                 jax.ShapeDtypeStruct((TAPS * half + 8, 4 * half), F32),
             ),
             in_specs=[hbm] * 5,
-            out_specs=[hbm, vmem, vmem],
+            out_specs=[hbm] * 3,
             scratch_shapes=[
                 pltpu.VMEM((4 * half, TAPS * lanes), F32),
                 pltpu.VMEM((4 * half, TAPS * lanes), F32),
@@ -414,23 +436,26 @@
         )(x_in, act_saved, d_out, w_one, w_two)
 
         depth = 8
-        d_x = pl.pallas_call(
+        d_x, grad_two, bias = pl.pallas_call(
             lambda *refs: unpack(num, *refs),
-            out_shape=jax.ShapeDtypeStruct((2, num, rows, width, half), BF16),
-            in_specs=[hbm],
-            out_specs=hbm,
+            out_shape=(
+                jax.ShapeDtypeStruct((2, num, rows, width, half), BF16),
+                jax.ShapeDtypeStruct((TAPS * half, 4 * half), F32),
+                jax.ShapeDtypeStruct((1, half), F32),
+            ),
+            in_specs=[hbm] * 2,
+            out_specs=[hbm] * 3,
             scratch_shapes=[
                 pltpu.VMEM((depth, rows, width, lanes), BF16),
                 pltpu.VMEM((depth, 2, rows, width, half), BF16),
-                dma((depth,)), dma((depth, 2)),
+                pltpu.VMEM((TAPS * half + 8, 4 * half), F32),
+                pltpu.VMEM((1, half), F32),
+                dma((depth,)), dma((depth, 2)), dma((2,)),
             ],
             cost_estimate=pl.CostEstimate(flops=10**10, bytes_accessed=5 * 10**7, transcendentals=0),
-        )(packed).reshape(x_in.shape)
-
+        )(packed, grad_two)
         grad_one = grad_one + lax.ppermute(grad_one, "sp", swap_rows)
-        bias = jnp.sum(grad_two[TAPS * half:, :half], axis=0)
-        grad_two = grad_two[:TAPS * half]
-        return d_x, grad_one.reshape(w_one.shape), grad_two.reshape(w_two.shape), bias
+        return d_x.reshape(x_in.shape), grad_one.reshape(w_one.shape), grad_two.reshape(w_two.shape), bias.reshape(half)
 
     act_spec = P("dp", "sp", None, "tp")
     kern_spec = P(None, None, "tp", None)

time: 764 us -> 759 us (level)
  no operation moved by 1% of the time
where the time goes in v4:
time: 759 us
  Pallas kernels  756 us (100%)
    pallas_call x1, Pallas kernels, local_step(): pl.pallas_call(lambda *refs: body(num, rows, width, *refs), out_shape=(ja...  739 us
    pallas_call x1, Pallas kernels, local_step(): pl.pallas_call(lambda *refs: unpack(num, *refs), out_shape=(jax.ShapeDtyp...  16.7 us
  transfers between devices with their start and end apart: 1, of which 0 were waited for; matrix products, arithmetic and copies ran while one was open for 0% of the time, Pallas kernels for 2%

profile of v4, /device:TPU:0, one launch (start us, length us, event | category | flops | bytes accessed | tf_op | source)
XLA Modules:
  0.0 758.7 jit_solution(12229679118355092864)
XLA Ops:
  0.6 739.2 %shard_map.84 = (bf16[32,64,32,128]{3,2,1,0:T(8,128)(2,1)}, f32[576,256]{1,0:T(8,128)}, f32[584,256]{1,0:T(8,128)}) custom-call(bf16[64,64,32,64]{3,2,1,0:T(8,128)(2,1)} %refs_0_.1, bf16[64,64,32,64]{3,2,1,0:T(8,128)(2,1)} %refs_1_.1, bf16[64,64,32,64]{3,2,1,0:T(8,128)(2,1)} %refs_2_.1, bf16[3,3,64,256]{3,2,1,0:T(8,128)(2,1)} %refs_3_.1, ...), custom_call_target="tpu_custom_call" | custom-call | tf_op jit(solution)/shard_map/pallas_call | solution.py:402
  739.9 0.0 copy-start
  739.9 1.2 collective-permute-start
  741.1 16.7 %shard_map.85 = (bf16[2,32,64,32,64]{4,3,2,1,0:T(8,128)(2,1)}, f32[576,256]{1,0:T(8,128)}, f32[1,64]{1,0:T(1,128)}) custom-call(bf16[32,64,32,128]{3,2,1,0:T(8,128)(2,1)} %get-tuple-element.10.refs_0_, f32[584,256]{1,0:T(8,128)} %get-tuple-element.11.refs_1_), custom_call_target="tpu_custom_call" | custom-call | flops 10000000000 | bytes 50000000 | tf_op jit(solution)/shard_map/pallas_call | solution.py:439
  757.8 0.0 collective-permute-done
  757.8 0.0 copy-done
  757.8 0.9 add.3
Async XLA Ops:
  739.9 17.9 %copy-start = (f32[576,256]{1,0:T(8,128)S(1)}, f32[576,256]{1,0:T(8,128)}, u32[]{:S(2)}) copy-start(f32[576,256]{1,0:T(8,128)} %get-tuple-element.13) | copy-start | bytes 1769476
  739.9 17.9 %collective-permute-start = (f32[576,256]{1,0:T(8,128)}, f32[576,256]{1,0:T(8,128)S(1)}, u32[]{:S(2)}, u32[]{:S(2)}) collective-permute-start(f32[576,256]{1,0:T(8,128)} %get-tuple-element.13), channel_id=1, source_target_pairs={{0,4},{4,0},{1,5},{5,1},{2,6},{6,2},{3,7},{7,3}} | collective-permute-start | bytes 1769480 | tf_op jit(solution)/shard_map/ppermute | solution.py:457

commit v5 on v4

--- a/solution.py
+++ b/solution.py
@@ -12,9 +12,9 @@
 GRAD_ROWS = 32
 
 
-def body(num, rows, width, x_hbm, a_hbm, y_hbm, w1_hbm, w2_hbm, dx_hbm, dw1_hbm, dw2_hbm,
-         acc1, acc2, db_ref, raw_own, raw_rem, weights, part_own, part_send, part_recv, row_recv, nat_own, nat_rem, g_own, g_oth, z_own, z_oth, shifted, out_own, out_rem,
-         load_sem, push_send, push_recv, g_send, g_recv, z_send, z_recv, out_sem, out_send, out_recv, raw_sem, raw_send, raw_recv, part_sems, free_sem):
+def body(num, rows, width, x_hbm, a_hbm, y_hbm, w1_ref, w2_ref, packed, dw1_ref, dw2_ref,
+         acc1, acc2, db_ref, raw_rem, weights, part_own, part_send, part_recv, row_recv, nat_own, nat_rem, g_own, g_oth, z_own, z_oth, shifted, out_own, out_rem,
+         load_sem, push_send, push_recv, g_send, g_recv, z_send, z_recv, out_send, out_recv, raw_send, raw_recv, part_sems, free_sem):
     dp, sp, tp = lax.axis_index("dp"), lax.axis_index("sp"), lax.axis_index("tp")
     core, chip = tp % 2, tp // 2
     partner = (dp, sp, tp + 1 - 2 * core)
@@ -70,9 +70,6 @@
         slot = img % 2
         return remote(out_own.at[slot], out_rem.at[slot], out_send.at[slot], out_recv.at[slot], partner)
 
-    def store_out(img):
-        return pltpu.make_async_copy(out_own.at[img % 2], dx_hbm.at[img], out_sem.at[img % 2])
-
     def finish_out(img):
         slot = img % 2
         swap_out(img).wait()
@@ -81,9 +78,7 @@
         def _(k):
             block = pl.ds(k * CONV_ROWS, CONV_ROWS)
             lane = lax.broadcasted_iota(jnp.int32, (CONV_ROWS, width, lanes), 2)
-            out_own[slot, block] = jnp.where(lane < half, out_own[slot, block], out_rem[slot, block])
-
-        store_out(img).start()
+            packed[img, block] = jnp.where(lane < half, out_own[slot, block], out_rem[slot, block])
 
     def dense(kind, slot, r0, count):
         mine = nat_own[kind, slot, pl.ds(r0, count)]
@@ -176,12 +171,10 @@
         side.wait()
         return forward
 
-    def raw_copies():
-        copies = []
-        for idx, src in enumerate((w1_hbm, w2_hbm)):
-            copies.append(pltpu.make_async_copy(src, raw_own.at[idx], raw_sem.at[idx]))
-            copies.append(remote(src, raw_rem.at[idx], raw_send.at[idx], raw_recv.at[idx], partner))
-        return copies
+    raw = (w1_ref, w2_ref)
+
+    def swap_raw(idx):
+        return remote(raw[idx], raw_rem.at[idx], raw_send.at[idx], raw_recv.at[idx], partner)
 
     def local_block(block):
         on_chip = chip if block < 2 else 1 - chip
@@ -189,13 +182,13 @@
         return pl.multiple_of((2 * on_chip + on_core) * half, half)
 
     def build_weights():
-        for copy in raw_copies():
-            copy.wait()
         for idx in range(2):
+            swap_raw(idx).wait()
+
             @pl.loop(0, 3)
             def _(kh):
                 for kw in range(3):
-                    taps = jnp.concatenate([raw_own[idx, kh, kw], raw_rem[idx, kh, kw]], axis=0).T
+                    taps = jnp.concatenate([raw[idx][kh, kw], raw_rem[idx, kh, kw]], axis=0).T
                     for block in range(4):
                         dst = pl.ds(pl.multiple_of(kh * 4 * half, half) + local_block(block), half)
                         weights[idx, dst, kw * lanes:(kw + 1) * lanes] = taps[block * half:(block + 1) * half]
@@ -222,8 +215,8 @@
         part_own[idx] += part_recv[idx]
 
     start_loads(0, 0)
-    for copy in raw_copies():
-        copy.start()
+    for idx in range(2):
+        swap_raw(idx).start()
     steps = num + 2
     zero_row = jnp.zeros((width, lanes), BF16)
     for slot in range(3):
@@ -300,10 +293,6 @@
             def _():
                 finish_out(img - 1)
 
-            @pl.when(img >= 2)
-            def _():
-                store_out(img - 2).wait()
-
             @pl.when(img == num - 2)
             def _():
                 add_part(1)
@@ -325,62 +314,39 @@
     swap_part(0).start()
     finish_out(num - 1)
     swap_rows().wait()
-    part_own[1] += row_recv[...]
-    second_grad = pltpu.make_async_copy(part_own.at[1], dw2_hbm, raw_sem.at[1])
-    second_grad.start()
-    add_part(0)
-    first_grad = pltpu.make_async_copy(part_own.at[0, pl.ds(0, grad_rows)], dw1_hbm, raw_sem.at[0])
-    first_grad.start()
-    store_out(num - 2).wait()
-    store_out(num - 1).wait()
-    second_grad.wait()
-    first_grad.wait()
-
-
-def unpack(num, packed_hbm, grad_hbm, out_hbm, grad_out, bias_out, packed, out, grad, bias, load_sem, store_sem, grad_sem):
+    dw2_ref[...] = part_own[1] + row_recv[...]
+    swap_part(0).wait()
+    inside = pl.ds(0, grad_rows)
+    dw1_ref[...] = part_own[0, inside] + part_recv[0, inside]
+
+
+def unpack(num, packed, grad, out_hbm, grad_out, bias_out, out, bias, store_sem, grad_sem):
     core = lax.axis_index("tp") % 2
-    depth, half = packed.shape[0], out.shape[-1]
-
-    def load(i):
-        slot = i % depth
-        return pltpu.make_async_copy(packed_hbm.at[i], packed.at[slot], load_sem.at[slot])
+    depth, half = out.shape[0], out.shape[-1]
 
     def stores(i):
         slot = i % depth
         return [pltpu.make_async_copy(out.at[slot, side], out_hbm.at[side, i], store_sem.at[slot, side]) for side in range(2)]
 
-    load_grad = pltpu.make_async_copy(grad_hbm, grad, grad_sem.at[0])
     store_grad = pltpu.make_async_copy(grad.at[pl.ds(0, TAPS * half)], grad_out, grad_sem.at[0])
     store_bias = pltpu.make_async_copy(bias, bias_out, grad_sem.at[1])
-    for i in range(depth):
-        load(i).start()
-    load_grad.start()
+    store_grad.start()
+    bias[...] = jnp.sum(grad[TAPS * half:, :half], axis=0, keepdims=True)
+    store_bias.start()
 
     @pl.loop(0, num)
     def _(i):
         slot = i % depth
-        load(i).wait()
-
-        @pl.when(i == depth)
-        def _():
-            load_grad.wait()
-            store_grad.start()
-            bias[...] = jnp.sum(grad[TAPS * half:, :half], axis=0, keepdims=True)
-            store_bias.start()
 
         @pl.when(i >= depth)
         def _():
             for copy in stores(i - depth):
                 copy.wait()
 
-        out[slot, core] = packed[slot, ..., :half]
-        out[slot, 1 - core] = packed[slot, ..., half:]
+        out[slot, core] = packed[i, ..., :half]
+        out[slot, 1 - core] = packed[i, ..., half:]
         for copy in stores(i):
             copy.start()
-
-        @pl.when(i + depth < num)
-        def _():
-            load(i + depth).start()
 
     for i in range(num - depth, num):
         for copy in stores(i):
@@ -399,6 +365,7 @@
         pad = (rows + 2, width, lanes)
         dma = pltpu.SemaphoreType.DMA
         hbm = pl.BlockSpec(memory_space=pltpu.HBM)
+        vmem = pl.BlockSpec(memory_space=pltpu.VMEM)
         packed, grad_one, grad_two = pl.pallas_call(
             lambda *refs: body(num, rows, width, *refs),
             out_shape=(
@@ -406,13 +373,12 @@
                 jax.ShapeDtypeStruct((TAPS * half, 4 * half), F32),
                 jax.ShapeDtypeStruct((TAPS * half + 8, 4 * half), F32),
             ),
-            in_specs=[hbm] * 5,
-            out_specs=[hbm] * 3,
+            in_specs=[hbm] * 3 + [vmem] * 2,
+            out_specs=[vmem] * 3,
             scratch_shapes=[
                 pltpu.VMEM((4 * half, TAPS * lanes), F32),
                 pltpu.VMEM((4 * half, TAPS * lanes), F32),
                 pltpu.VMEM((8, lanes), F32),
-                pltpu.VMEM((2,) + w_one.shape, BF16),
                 pltpu.VMEM((2,) + w_one.shape, BF16),
                 pltpu.VMEM((2, 3 * 4 * half, 3 * lanes), BF16),
                 part, part, part,
@@ -428,11 +394,11 @@
                 pltpu.VMEM((2, rows, width, lanes), BF16),
                 dma((3, 2)), dma((3, 2)), dma((3, 2)),
                 dma((3, 2)), dma((3, 2)), dma((3, 2)), dma((3, 2)),
-                dma((2,)), dma((2,)), dma((2,)),
-                dma((2,)), dma((2,)), dma((2,)), dma((3, 2)),
+                dma((2,)), dma((2,)),
+                dma((2,)), dma((2,)), dma((3, 2)),
                 pltpu.SemaphoreType.REGULAR((3,)),
             ],
-            compiler_params=pltpu.CompilerParams(collective_id=0, has_side_effects=True, vmem_limit_bytes=60 * 1024 * 1024),
+            compiler_params=pltpu.CompilerParams(collective_id=0, has_side_effects=True, vmem_limit_bytes=30 * 1024 * 1024),
         )(x_in, act_saved, d_out, w_one, w_two)
 
         depth = 8
@@ -443,15 +409,14 @@
                 jax.ShapeDtypeStruct((TAPS * half, 4 * half), F32),
                 jax.ShapeDtypeStruct((1, half), F32),
             ),
-            in_specs=[hbm] * 2,
+            in_specs=[vmem] * 2,
             out_specs=[hbm] * 3,
             scratch_shapes=[
-                pltpu.VMEM((depth, rows, width, lanes), BF16),
                 pltpu.VMEM((depth, 2, rows, width, half), BF16),
-                pltpu.VMEM((TAPS * half + 8, 4 * half), F32),
                 pltpu.VMEM((1, half), F32),
-                dma((depth,)), dma((depth, 2)), dma((2,)),
+                dma((depth, 2)), dma((2,)),
             ],
+            compiler_params=pltpu.CompilerParams(vmem_limit_bytes=14 * 1024 * 1024),
             cost_estimate=pl.CostEstimate(flops=10**10, bytes_accessed=5 * 10**7, transcendentals=0),
         )(packed, grad_two)
         grad_one = grad_one + lax.ppermute(grad_one, "sp", swap_rows)

time: 759 us -> 757 us (level)
  transfers between devices with their start and end apart: 1 -> 1, of which waited for: 0 -> 1; matrix products, arithmetic and copies ran while one was open for 0% -> 0% of each run, Pallas kernels for 2% -> 2%
where the time goes in v5:
time: 757 us
  Pallas kernels  751 us (99%)
    pallas_call x1, Pallas kernels, local_step(): pl.pallas_call(lambda *refs: body(num, rows, width, *refs), out_shape=(ja...  738 us
  transfers between devices with their start and end apart: 1, of which 1 were waited for; matrix products, arithmetic and copies ran while one was open for 0% of the time, Pallas kernels for 2%

profile of v5, /device:TPU:0, one launch (start us, length us, event | category | flops | bytes accessed | tf_op | source)
XLA Modules:
  0.0 757.2 jit_solution(6954130784726628182)
XLA Ops:
  0.6 0.0 copy-start
  0.6 1.0 copy-done
  1.6 0.0 copy-start.1
  1.6 1.0 copy-done.1
  2.6 738.3 %shard_map.84 = (bf16[32,64,32,128]{3,2,1,0:T(8,128)(2,1)S(1)}, f32[576,256]{1,0:T(8,128)S(1)}, f32[584,256]{1,0:T(8,128)S(1)}) custom-call(bf16[64,64,32,64]{3,2,1,0:T(8,128)(2,1)} %refs_0_.1, bf16[64,64,32,64]{3,2,1,0:T(8,128)(2,1)} %refs_1_.1, bf16[64,64,32,64]{3,2,1,0:T(8,128)(2,1)} %refs_2_.1, bf16[3,3,64,256]{3,2,1,0:T(8,128)(2,1)S(1)} %copy-done, ...), custom_call_target="tpu_custom_call" | custom-call | tf_op jit(solution)/shard_map/pallas_call | solution.py:369
  740.9 1.2 collective-permute-start
  742.1 12.6 %shard_map.85 = (bf16[2,32,64,32,64]{4,3,2,1,0:T(8,128)(2,1)}, f32[576,256]{1,0:T(8,128)}, f32[1,64]{1,0:T(1,128)}) custom-call(bf16[32,64,32,128]{3,2,1,0:T(8,128)(2,1)S(1)} %get-tuple-element.10.refs_0_, f32[584,256]{1,0:T(8,128)S(1)} %get-tuple-element.11.refs_1_), custom_call_target="tpu_custom_call" | custom-call | flops 10000000000 | bytes 50000000 | tf_op jit(solution)/shard_map/pallas_call | solution.py:405
  754.7 1.6 collective-permute-done
  756.3 0.9 add.3
Async XLA Ops:
  0.6 1.0 copy-start
  1.6 1.0 copy-start.1
  740.9 15.4 %collective-permute-start = (f32[576,256]{1,0:T(8,128)S(1)}, f32[576,256]{1,0:T(8,128)S(1)}, u32[]{:S(2)}, u32[]{:S(2)}) collective-permute-start(f32[576,256]{1,0:T(8,128)S(1)} %get-tuple-element.13), channel_id=1, source_target_pairs={{0,4},{4,0},{1,5},{5,1},{2,6},{6,2},{3,7},{7,3}} | collective-permute-start | bytes 1769480 | tf_op jit(solution)/shard_map/ppermute | solution.py:422

commit v6 on v5

--- a/solution.py
+++ b/solution.py
@@ -12,7 +12,7 @@
 GRAD_ROWS = 32
 
 
-def body(num, rows, width, x_hbm, a_hbm, y_hbm, w1_ref, w2_ref, packed, dw1_ref, dw2_ref,
+def body(num, rows, width, x_hbm, a_hbm, y_hbm, w1_ref, w2_ref, packed, dw1_ref, dw1_rest_ref, dw2_ref,
          acc1, acc2, db_ref, raw_rem, weights, part_own, part_send, part_recv, row_recv, nat_own, nat_rem, g_own, g_oth, z_own, z_oth, shifted, out_own, out_rem,
          load_sem, push_send, push_recv, g_send, g_recv, z_send, z_recv, out_send, out_recv, raw_send, raw_recv, part_sems, free_sem):
     dp, sp, tp = lax.axis_index("dp"), lax.axis_index("sp"), lax.axis_index("tp")
@@ -114,12 +114,15 @@
         out = jnp.dot(lhs, w_ref[...], preferred_element_type=F32)
         return out[:, lanes:2 * lanes] + from_right(out[:, :lanes]) + from_left(out[:, 2 * lanes:])
 
-    def kgrad(own, oth, acc):
+    def kgrad(sources, acc, first_row):
+        dst = pl.ds(first_row, lanes * len(sources))
+
         def piece(r, count):
-            lhs = jnp.concatenate(both(own, oth, r, count), axis=-1)
-            taps = [shifted[kw, pl.ds(r + kh, count)].reshape(count * width, lanes) for kh in range(3) for kw in range(3)]
+            shape = (count * width, lanes)
+            lhs = jnp.concatenate([src[pl.ds(r, count)].reshape(shape) for src in sources], axis=-1)
+            taps = [shifted[kw, pl.ds(r + kh, count)].reshape(shape) for kh in range(3) for kw in range(3)]
             rhs = jnp.concatenate(taps, axis=-1)
-            acc[...] += lax.dot_general(lhs, rhs, (((0,), (0,)), ((), ())), preferred_element_type=F32)
+            acc[dst] += lax.dot_general(lhs, rhs, (((0,), (0,)), ((), ())), preferred_element_type=F32)
 
         def inner():
             @pl.loop(0, rows // GRAD_ROWS)
@@ -165,10 +168,9 @@
         blocks(halo, step)
 
     def arrive(copies):
-        main, side, forward = copies
+        main, _, forward = copies
         main.wait()
         forward.start()
-        side.wait()
         return forward
 
     raw = (w1_ref, w2_ref)
@@ -195,24 +197,29 @@
 
     grad_rows = TAPS * half
 
-    def collect(acc, idx):
+    def collect(acc, side, idx):
         @pl.loop(0, TAPS)
         def _(tap):
             cols = pl.ds(pl.multiple_of(tap * lanes, lanes), lanes)
-            flipped = jnp.concatenate([acc[pl.ds(local_block(block), half), cols] for block in range(4)], axis=0).T
+            firsts = (core, 1 - core)
+            pieces = [acc[pl.ds(pl.multiple_of(side * lanes + first * half, half), half), cols] for first in firsts]
+            flipped = jnp.concatenate(pieces, axis=0).T
             dst = pl.ds(pl.multiple_of(tap * half, half), half)
             part_own[idx, dst] = flipped[:half]
             part_send[idx, dst] = flipped[half:]
 
-    def swap_part(idx):
-        return remote(part_send.at[idx], part_recv.at[idx], part_sems.at[idx, 0], part_sems.at[idx, 1], partner)
-
-    def swap_rows():
-        return remote(part_own.at[1], row_recv, part_sems.at[2, 0], part_sems.at[2, 1], beside)
-
-    def add_part(idx):
-        swap_part(idx).wait()
-        part_own[idx] += part_recv[idx]
+    def swap_part(lo, count):
+        which = pl.ds(lo, count)
+        return remote(part_send.at[which], part_recv.at[which], part_sems.at[0, lo], part_sems.at[1, lo], partner)
+
+    def swap_rows(lo, count):
+        which = pl.ds(lo, count)
+        return remote(part_own.at[which], row_recv.at[which], part_sems.at[2, lo], part_sems.at[3, lo], beside)
+
+    def add_part(lo, count):
+        swap_part(lo, count).wait()
+        which = pl.ds(lo, count)
+        part_own[which] += part_recv[which]
 
     start_loads(0, 0)
     for idx in range(2):
@@ -229,9 +236,9 @@
         for row in (0, 1, rows + 2, rows + 3):
             shifted[side, row] = zero_row
     tail = pl.ds(grad_rows, 8)
-    for idx in range(2):
-        part_own[idx, tail] = jnp.zeros((8, 2 * lanes), F32)
-        part_send[idx, tail] = jnp.zeros((8, 2 * lanes), F32)
+    for idx in range(4):
+        part_own[idx, tail] = jnp.zeros((8, lanes), F32)
+        part_send[idx, tail] = jnp.zeros((8, lanes), F32)
 
     @pl.loop(0, steps)
     def _(step):
@@ -270,18 +277,22 @@
             start_loads(2, img)
             wait_loads(1, img)
             prepare(1, img)
-            first(img, arrive(g_exchange(img)))
+            copies = g_exchange(img)
+            halo = arrive(copies)
+            copies[1].wait()
+            first(img, halo)
             for copy in z_exchange(img)[:2]:
                 copy.start()
-            for part in kgrad(g_own.at[img % 3], g_oth.at[img % 2], acc2):
+            for part in kgrad((g_own.at[img % 3], g_oth.at[img % 2]), acc2, 0):
                 part()
 
             @pl.when(img == num - 1)
             def _():
-                collect(acc2, 1)
-                part_own[1, tail, :lanes] = db_ref[...]
-                part_send[1, tail, :lanes] = pltpu.roll(db_ref[...], half, 1)
-                swap_part(1).start()
+                collect(acc2, 0, 2)
+                collect(acc2, 1, 3)
+                part_own[2, tail] = db_ref[...]
+                part_send[2, tail] = pltpu.roll(db_ref[...], half, 1)
+                swap_part(2, 2).start()
 
         @pl.when(step >= 2)
         def _():
@@ -295,11 +306,23 @@
 
             @pl.when(img == num - 2)
             def _():
-                add_part(1)
-                swap_rows().start()
-
-            halo = arrive(z_exchange(img))
-            inner, outer = kgrad(z_own.at[img % 2], z_oth.at[img % 2], acc1)
+                add_part(2, 2)
+                swap_rows(2, 2).start()
+
+            copies = z_exchange(img)
+            copies[1].wait()
+            for part in kgrad((z_own.at[img % 2],), acc1, 0):
+                part()
+
+            @pl.when(img == num - 1)
+            def _():
+                collect(acc1, 0, 0)
+                swap_part(0, 1).start()
+                add_part(0, 1)
+                swap_rows(0, 1).start()
+
+            halo = arrive(copies)
+            inner, outer = kgrad((z_oth.at[img % 2],), acc1, lanes)
             inner()
             second(img, halo)
             swap_out(img).start()
@@ -310,14 +333,16 @@
             for rel, peer in enumerate(peers):
                 pl.semaphore_signal(free_sem.at[rel], inc=1, device_id=peer, device_id_type=MESH)
 
-    collect(acc1, 0)
-    swap_part(0).start()
+    collect(acc1, 1, 1)
+    swap_part(1, 1).start()
     finish_out(num - 1)
-    swap_rows().wait()
-    dw2_ref[...] = part_own[1] + row_recv[...]
-    swap_part(0).wait()
+    swap_rows(2, 2).wait()
+    dw2_ref[...] = part_own[pl.ds(2, 2)] + row_recv[pl.ds(2, 2)]
+    swap_rows(0, 1).wait()
     inside = pl.ds(0, grad_rows)
-    dw1_ref[...] = part_own[0, inside] + part_recv[0, inside]
+    dw1_ref[...] = part_own[0, inside] + row_recv[0, inside]
+    swap_part(1, 1).wait()
+    dw1_rest_ref[...] = part_own[1, inside] + part_recv[1, inside]
 
 
 def unpack(num, packed, grad, out_hbm, grad_out, bias_out, out, bias, store_sem, grad_sem):
@@ -328,10 +353,16 @@
         slot = i % depth
         return [pltpu.make_async_copy(out.at[slot, side], out_hbm.at[side, i], store_sem.at[slot, side]) for side in range(2)]
 
-    store_grad = pltpu.make_async_copy(grad.at[pl.ds(0, TAPS * half)], grad_out, grad_sem.at[0])
-    store_bias = pltpu.make_async_copy(bias, bias_out, grad_sem.at[1])
-    store_grad.start()
-    bias[...] = jnp.sum(grad[TAPS * half:, :half], axis=0, keepdims=True)
+    chip = lax.axis_index("tp") // 2
+    inside = pl.ds(0, TAPS * half)
+    store_grads = [
+        pltpu.make_async_copy(grad.at[side, inside], grad_out.at[:, pl.ds(tile * 2 * half, 2 * half)], grad_sem.at[tile])
+        for tile, side in enumerate((chip, 1 - chip))
+    ]
+    store_bias = pltpu.make_async_copy(bias, bias_out, grad_sem.at[2])
+    for copy in store_grads:
+        copy.start()
+    bias[...] = jnp.sum(grad[0, TAPS * half:, :half], axis=0, keepdims=True)
     store_bias.start()
 
     @pl.loop(0, num)
@@ -351,8 +382,8 @@
     for i in range(num - depth, num):
         for copy in stores(i):
             copy.wait()
-    store_grad.wait()
-    store_bias.wait()
+    for copy in store_grads + [store_bias]:
+        copy.wait()
 
 
 def solution(mesh):
@@ -361,28 +392,28 @@
         num = images // 2
         lanes = 2 * half
         swap_rows = [(0, 1), (1, 0)]
-        part = pltpu.VMEM((2, TAPS * half + 8, 4 * half), F32)
+        part = pltpu.VMEM((4, TAPS * half + 8, lanes), F32)
         pad = (rows + 2, width, lanes)
         dma = pltpu.SemaphoreType.DMA
         hbm = pl.BlockSpec(memory_space=pltpu.HBM)
         vmem = pl.BlockSpec(memory_space=pltpu.VMEM)
-        packed, grad_one, grad_two = pl.pallas_call(
+        packed, near, far, grad_two = pl.pallas_call(
             lambda *refs: body(num, rows, width, *refs),
             out_shape=(
                 jax.ShapeDtypeStruct((num, rows, width, lanes), BF16),
-                jax.ShapeDtypeStruct((TAPS * half, 4 * half), F32),
-                jax.ShapeDtypeStruct((TAPS * half + 8, 4 * half), F32),
+                jax.ShapeDtypeStruct((TAPS * half, lanes), F32),
+                jax.ShapeDtypeStruct((TAPS * half, lanes), F32),
+                jax.ShapeDtypeStruct((2, TAPS * half + 8, lanes), F32),
             ),
             in_specs=[hbm] * 3 + [vmem] * 2,
-            out_specs=[vmem] * 3,
+            out_specs=[vmem] * 4,
             scratch_shapes=[
                 pltpu.VMEM((4 * half, TAPS * lanes), F32),
                 pltpu.VMEM((4 * half, TAPS * lanes), F32),
                 pltpu.VMEM((8, lanes), F32),
                 pltpu.VMEM((2,) + w_one.shape, BF16),
                 pltpu.VMEM((2, 3 * 4 * half, 3 * lanes), BF16),
-                part, part, part,
-                pltpu.VMEM((TAPS * half + 8, 4 * half), F32),
+                part, part, part, part,
                 pltpu.VMEM((3, 2, rows, width, half), BF16),
                 pltpu.VMEM((3, 2, rows, width, half), BF16),
                 pltpu.VMEM((3,) + pad, BF16),
@@ -395,7 +426,7 @@
                 dma((3, 2)), dma((3, 2)), dma((3, 2)),
                 dma((3, 2)), dma((3, 2)), dma((3, 2)), dma((3, 2)),
                 dma((2,)), dma((2,)),
-                dma((2,)), dma((2,)), dma((3, 2)),
+                dma((2,)), dma((2,)), dma((4, 4)),
                 pltpu.SemaphoreType.REGULAR((3,)),
             ],
             compiler_params=pltpu.CompilerParams(collective_id=0, has_side_effects=True, vmem_limit_bytes=30 * 1024 * 1024),
@@ -414,12 +445,14 @@
             scratch_shapes=[
                 pltpu.VMEM((depth, 2, rows, width, half), BF16),
                 pltpu.VMEM((1, half), F32),
-                dma((depth, 2)), dma((2,)),
+                dma((depth, 2)), dma((3,)),
             ],
             compiler_params=pltpu.CompilerParams(vmem_limit_bytes=14 * 1024 * 1024),
             cost_estimate=pl.CostEstimate(flops=10**10, bytes_accessed=5 * 10**7, transcendentals=0),
         )(packed, grad_two)
-        grad_one = grad_one + lax.ppermute(grad_one, "sp", swap_rows)
+        far = far + lax.ppermute(far, "sp", swap_rows)
+        on_left = lax.axis_index("tp") < 2
+        grad_one = jnp.concatenate([jnp.where(on_left, near, far), jnp.where(on_left, far, near)], axis=1)
         return d_x.reshape(x_in.shape), grad_one.reshape(w_one.shape), grad_two.reshape(w_two.shape), bias.reshape(half)
 
     act_spec = P("dp", "sp", None, "tp")

time: 757 us -> 765 us (1.011)
  Pallas kernels: 751 us -> 760 us
    pallas_call x1, Pallas kernels: 738 us -> 748 us  [local_step(): pl.pallas_call(lambda *refs: body(num, rows, width, *refs), out_shape=(ja...]
  transfers between devices with their start and end apart: 1 -> 1, of which waited for: 1 -> 0; matrix products, arithmetic and copies ran while one was open for 0% -> 0% of each run, Pallas kernels for 2% -> 2%
where the time goes in v6:
time: 765 us; the launch traced here: 764 us
  Pallas kernels  760 us (99%)
    pallas_call x1, Pallas kernels, local_step(): pl.pallas_call(lambda *refs: body(num, rows, width, *refs), out_shape=(ja...  748 us
  transfers between devices with their start and end apart: 1, of which 0 were waited for; matrix products, arithmetic and copies ran while one was open for 0% of the time, Pallas kernels for 2%

profile of v6, /device:TPU:0, one launch (start us, length us, event | category | flops | bytes accessed | tf_op | source)
XLA Modules:
  0.0 764.5 jit_solution(12900235014748453433)
XLA Ops:
  0.6 0.0 copy-start
  0.6 1.0 copy-done
  1.6 0.0 copy-start.1
  1.6 1.0 copy-done.1
  2.6 747.6 %shard_map.84 = (bf16[32,64,32,128]{3,2,1,0:T(8,128)(2,1)S(1)}, f32[576,128]{1,0:T(8,128)S(1)}, f32[576,128]{1,0:T(8,128)S(1)}, f32[2,584,128]{2,1,0:T(8,128)S(1)}) custom-call(bf16[64,64,32,64]{3,2,1,0:T(8,128)(2,1)} %refs_0_.1, bf16[64,64,32,64]{3,2,1,0:T(8,128)(2,1)} %refs_1_.1, bf16[64,64,32,64]{3,2,1,0:T(8,128)(2,1)} %refs_2_.1, ...), custom_call_target="tpu_custom_call" | custom-call | tf_op jit(solution)/shard_map/pallas_call | solution.py:400
  750.2 0.7 collective-permute-start
  750.9 12.6 %shard_map.85 = (bf16[2,32,64,32,64]{4,3,2,1,0:T(8,128)(2,1)}, f32[576,256]{1,0:T(8,128)}, f32[1,64]{1,0:T(1,128)}) custom-call(bf16[32,64,32,128]{3,2,1,0:T(8,128)(2,1)S(1)} %get-tuple-element.11.refs_0_, f32[2,584,128]{2,1,0:T(8,128)S(1)} %get-tuple-element.12.refs_1_), custom_call_target="tpu_custom_call" | custom-call | flops 10000000000 | bytes 50000000 | tf_op jit(solution)/shard_map/pallas_call | solution.py:436
  763.6 0.0 collective-permute-done
  763.6 0.1 broadcast_select_fusion.1
  763.6 0.9 pad_maximum_fusion
Async XLA Ops:
  0.6 1.0 copy-start
  1.6 1.0 copy-start.1
  750.2 13.4 %collective-permute-start = (f32[576,128]{1,0:T(8,128)S(1)}, f32[576,128]{1,0:T(8,128)S(1)}, u32[]{:S(2)}, u32[]{:S(2)}) collective-permute-start(f32[576,128]{1,0:T(8,128)S(1)} %get-tuple-element.15), channel_id=1, source_target_pairs={{0,4},{4,0},{1,5},{5,1},{2,6},{6,2},{3,7},{7,3}} | collective-permute-start | bytes 884744 | tf_op jit(solution)/shard_map/ppermute | solution.py:453

commit v7 on v6

--- a/solution.py
+++ b/solution.py
@@ -212,9 +212,14 @@
         which = pl.ds(lo, count)
         return remote(part_send.at[which], part_recv.at[which], part_sems.at[0, lo], part_sems.at[1, lo], partner)
 
-    def swap_rows(lo, count):
-        which = pl.ds(lo, count)
-        return remote(part_own.at[which], row_recv.at[which], part_sems.at[2, lo], part_sems.at[3, lo], beside)
+    third = grad_rows // 3
+    whole = grad_rows + 8
+    row_pieces = ((2, 0, whole), (3, 0, whole), (0, 0, third), (0, third, third), (0, 2 * third, third))
+
+    def swap_rows(piece):
+        idx, start, count = row_pieces[piece]
+        which = pl.ds(start, count)
+        return remote(part_own.at[idx, which], row_recv.at[idx, which], part_sems.at[2, piece], part_sems.at[3, piece], beside)
 
     def add_part(lo, count):
         swap_part(lo, count).wait()
@@ -307,7 +312,7 @@
             @pl.when(img == num - 2)
             def _():
                 add_part(2, 2)
-                swap_rows(2, 2).start()
+                swap_rows(0).start()
 
             copies = z_exchange(img)
             copies[1].wait()
@@ -319,9 +324,19 @@
                 collect(acc1, 0, 0)
                 swap_part(0, 1).start()
                 add_part(0, 1)
-                swap_rows(0, 1).start()
+                swap_rows(2).start()
 
             halo = arrive(copies)
+
+            @pl.when(img == num - 2)
+            def _():
+                swap_rows(1).start()
+
+            @pl.when(img == num - 1)
+            def _():
+                swap_rows(3).start()
+                swap_rows(4).start()
+
             inner, outer = kgrad((z_oth.at[img % 2],), acc1, lanes)
             inner()
             second(img, halo)
@@ -336,13 +351,15 @@
     collect(acc1, 1, 1)
     swap_part(1, 1).start()
     finish_out(num - 1)
-    swap_rows(2, 2).wait()
+    swap_rows(0).wait()
+    swap_rows(1).wait()
     dw2_ref[...] = part_own[pl.ds(2, 2)] + row_recv[pl.ds(2, 2)]
-    swap_rows(0, 1).wait()
     inside = pl.ds(0, grad_rows)
-    dw1_ref[...] = part_own[0, inside] + row_recv[0, inside]
     swap_part(1, 1).wait()
     dw1_rest_ref[...] = part_own[1, inside] + part_recv[1, inside]
+    for piece in range(2, 5):
+        swap_rows(piece).wait()
+    dw1_ref[...] = part_own[0, inside] + row_recv[0, inside]
 
 
 def unpack(num, packed, grad, out_hbm, grad_out, bias_out, out, bias, store_sem, grad_sem):
@@ -426,7 +443,7 @@
                 dma((3, 2)), dma((3, 2)), dma((3, 2)),
                 dma((3, 2)), dma((3, 2)), dma((3, 2)), dma((3, 2)),
                 dma((2,)), dma((2,)),
-                dma((2,)), dma((2,)), dma((4, 4)),
+                dma((2,)), dma((2,)), dma((4, 5)),
                 pltpu.SemaphoreType.REGULAR((3,)),
             ],
             compiler_params=pltpu.CompilerParams(collective_id=0, has_side_effects=True, vmem_limit_bytes=30 * 1024 * 1024),

time: 765 us -> 756 us (0.988)
  Pallas kernels: 760 us -> 751 us
    pallas_call x1, Pallas kernels: 748 us -> 739 us  [local_step(): pl.pallas_call(lambda *refs: body(num, rows, width, *refs), out_shape=(ja...]
where the time goes in v7:
time: 756 us; the launch traced here: 755 us
  Pallas kernels  751 us (99%)
    pallas_call x1, Pallas kernels, local_step(): pl.pallas_call(lambda *refs: body(num, rows, width, *refs), out_shape=(ja...  739 us
  transfers between devices with their start and end apart: 1, of which 0 were waited for; matrix products, arithmetic and copies ran while one was open for 0% of the time, Pallas kernels for 2%

profile of v7, /device:TPU:0, one launch (start us, length us, event | category | flops | bytes accessed | tf_op | source)
XLA Modules:
  0.0 755.4 jit_solution(7803641542139124700)
XLA Ops:
  0.6 0.0 copy-start
  0.6 1.0 copy-done
  1.6 0.0 copy-start.1
  1.6 1.0 copy-done.1
  2.6 738.5 %shard_map.84 = (bf16[32,64,32,128]{3,2,1,0:T(8,128)(2,1)S(1)}, f32[576,128]{1,0:T(8,128)S(1)}, f32[576,128]{1,0:T(8,128)S(1)}, f32[2,584,128]{2,1,0:T(8,128)S(1)}) custom-call(bf16[64,64,32,64]{3,2,1,0:T(8,128)(2,1)} %refs_0_.1, bf16[64,64,32,64]{3,2,1,0:T(8,128)(2,1)} %refs_1_.1, bf16[64,64,32,64]{3,2,1,0:T(8,128)(2,1)} %refs_2_.1, ...), custom_call_target="tpu_custom_call" | custom-call | tf_op jit(solution)/shard_map/pallas_call | solution.py:417
  741.1 0.7 collective-permute-start
  741.8 12.6 %shard_map.85 = (bf16[2,32,64,32,64]{4,3,2,1,0:T(8,128)(2,1)}, f32[576,256]{1,0:T(8,128)}, f32[1,64]{1,0:T(1,128)}) custom-call(bf16[32,64,32,128]{3,2,1,0:T(8,128)(2,1)S(1)} %get-tuple-element.11.refs_0_, f32[2,584,128]{2,1,0:T(8,128)S(1)} %get-tuple-element.12.refs_1_), custom_call_target="tpu_custom_call" | custom-call | flops 10000000000 | bytes 50000000 | tf_op jit(solution)/shard_map/pallas_call | solution.py:453
  754.4 0.0 collective-permute-done
  754.5 0.1 broadcast_select_fusion.1
  754.5 0.9 pad_maximum_fusion
Async XLA Ops:
  0.6 1.0 copy-start
  1.6 1.0 copy-start.1
  741.1 13.4 %collective-permute-start = (f32[576,128]{1,0:T(8,128)S(1)}, f32[576,128]{1,0:T(8,128)S(1)}, u32[]{:S(2)}, u32[]{:S(2)}) collective-permute-start(f32[576,128]{1,0:T(8,128)S(1)} %get-tuple-element.15), channel_id=1, source_target_pairs={{0,4},{4,0},{1,5},{5,1},{2,6},{6,2},{3,7},{7,3}} | collective-permute-start | bytes 884744 | tf_op jit(solution)/shard_map/ppermute | solution.py:470

commit v8 on v7

--- a/solution.py
+++ b/solution.py
@@ -12,9 +12,9 @@
 GRAD_ROWS = 32
 
 
-def body(num, rows, width, x_hbm, a_hbm, y_hbm, w1_ref, w2_ref, packed, dw1_ref, dw1_rest_ref, dw2_ref,
-         acc1, acc2, db_ref, raw_rem, weights, part_own, part_send, part_recv, row_recv, nat_own, nat_rem, g_own, g_oth, z_own, z_oth, shifted, out_own, out_rem,
-         load_sem, push_send, push_recv, g_send, g_recv, z_send, z_recv, out_send, out_recv, raw_send, raw_recv, part_sems, free_sem):
+def body(num, rows, width, x_hbm, a_hbm, y_hbm, w1_hbm, w2_hbm, packed, dw1_ref, dw1_rest_ref, dw2_ref,
+         acc1, acc2, db_ref, raw_own, raw_rem, weights, part_own, part_send, part_recv, row_recv, nat_own, nat_rem, g_own, g_oth, z_own, z_oth, shifted, out_own, out_rem,
+         load_sem, push_send, push_recv, g_send, g_recv, z_send, z_recv, out_send, out_recv, raw_sem, raw_send, raw_recv, part_sems, free_sem):
     dp, sp, tp = lax.axis_index("dp"), lax.axis_index("sp"), lax.axis_index("tp")
     core, chip = tp % 2, tp // 2
     partner = (dp, sp, tp + 1 - 2 * core)
@@ -173,10 +173,13 @@
         forward.start()
         return forward
 
-    raw = (w1_ref, w2_ref)
+    raw = (w1_hbm, w2_hbm)
 
     def swap_raw(idx):
         return remote(raw[idx], raw_rem.at[idx], raw_send.at[idx], raw_recv.at[idx], partner)
+
+    def load_raw(idx):
+        return pltpu.make_async_copy(raw[idx], raw_own.at[idx], raw_sem.at[idx])
 
     def local_block(block):
         on_chip = chip if block < 2 else 1 - chip
@@ -185,12 +188,13 @@
 
     def build_weights():
         for idx in range(2):
+            load_raw(idx).wait()
             swap_raw(idx).wait()
 
             @pl.loop(0, 3)
             def _(kh):
                 for kw in range(3):
-                    taps = jnp.concatenate([raw[idx][kh, kw], raw_rem[idx, kh, kw]], axis=0).T
+                    taps = jnp.concatenate([raw_own[idx, kh, kw], raw_rem[idx, kh, kw]], axis=0).T
                     for block in range(4):
                         dst = pl.ds(pl.multiple_of(kh * 4 * half, half) + local_block(block), half)
                         weights[idx, dst, kw * lanes:(kw + 1) * lanes] = taps[block * half:(block + 1) * half]
@@ -214,7 +218,7 @@
 
     third = grad_rows // 3
     whole = grad_rows + 8
-    row_pieces = ((2, 0, whole), (3, 0, whole), (0, 0, third), (0, third, third), (0, 2 * third, third))
+    row_pieces = ((2, 0, whole), (3, 0, whole), (0, 0, third), (0, third, third))
 
     def swap_rows(piece):
         idx, start, count = row_pieces[piece]
@@ -228,6 +232,7 @@
 
     start_loads(0, 0)
     for idx in range(2):
+        load_raw(idx).start()
         swap_raw(idx).start()
     steps = num + 2
     zero_row = jnp.zeros((width, lanes), BF16)
@@ -335,7 +340,6 @@
             @pl.when(img == num - 1)
             def _():
                 swap_rows(3).start()
-                swap_rows(4).start()
 
             inner, outer = kgrad((z_oth.at[img % 2],), acc1, lanes)
             inner()
@@ -354,12 +358,14 @@
     swap_rows(0).wait()
     swap_rows(1).wait()
     dw2_ref[...] = part_own[pl.ds(2, 2)] + row_recv[pl.ds(2, 2)]
+    done, late = pl.ds(0, 2 * third), pl.ds(2 * third, third)
+    dw1_rest_ref[pl.ds(0, third)] = part_own[0, late]
+    swap_part(1, 1).wait()
     inside = pl.ds(0, grad_rows)
-    swap_part(1, 1).wait()
-    dw1_rest_ref[...] = part_own[1, inside] + part_recv[1, inside]
-    for piece in range(2, 5):
-        swap_rows(piece).wait()
-    dw1_ref[...] = part_own[0, inside] + row_recv[0, inside]
+    dw1_rest_ref[pl.ds(third, grad_rows)] = part_own[1, inside] + part_recv[1, inside]
+    swap_rows(2).wait()
+    swap_rows(3).wait()
+    dw1_ref[...] = part_own[0, done] + row_recv[0, done]
 
 
 def unpack(num, packed, grad, out_hbm, grad_out, bias_out, out, bias, store_sem, grad_sem):
@@ -409,25 +415,27 @@
         num = images // 2
         lanes = 2 * half
         swap_rows = [(0, 1), (1, 0)]
+        third = TAPS * half // 3
         part = pltpu.VMEM((4, TAPS * half + 8, lanes), F32)
         pad = (rows + 2, width, lanes)
         dma = pltpu.SemaphoreType.DMA
         hbm = pl.BlockSpec(memory_space=pltpu.HBM)
         vmem = pl.BlockSpec(memory_space=pltpu.VMEM)
-        packed, near, far, grad_two = pl.pallas_call(
+        packed, near, rest, grad_two = pl.pallas_call(
             lambda *refs: body(num, rows, width, *refs),
             out_shape=(
                 jax.ShapeDtypeStruct((num, rows, width, lanes), BF16),
-                jax.ShapeDtypeStruct((TAPS * half, lanes), F32),
-                jax.ShapeDtypeStruct((TAPS * half, lanes), F32),
+                jax.ShapeDtypeStruct((TAPS * half - third, lanes), F32),
+                jax.ShapeDtypeStruct((TAPS * half + third, lanes), F32),
                 jax.ShapeDtypeStruct((2, TAPS * half + 8, lanes), F32),
             ),
-            in_specs=[hbm] * 3 + [vmem] * 2,
+            in_specs=[hbm] * 5,
             out_specs=[vmem] * 4,
             scratch_shapes=[
                 pltpu.VMEM((4 * half, TAPS * lanes), F32),
                 pltpu.VMEM((4 * half, TAPS * lanes), F32),
                 pltpu.VMEM((8, lanes), F32),
+                pltpu.VMEM((2,) + w_one.shape, BF16),
                 pltpu.VMEM((2,) + w_one.shape, BF16),
                 pltpu.VMEM((2, 3 * 4 * half, 3 * lanes), BF16),
                 part, part, part, part,
@@ -443,11 +451,11 @@
                 dma((3, 2)), dma((3, 2)), dma((3, 2)),
                 dma((3, 2)), dma((3, 2)), dma((3, 2)), dma((3, 2)),
                 dma((2,)), dma((2,)),
-                dma((2,)), dma((2,)), dma((4, 5)),
+                dma((2,)), dma((2,)), dma((2,)), dma((4, 4)),
                 pltpu.SemaphoreType.REGULAR((3,)),
             ],
-            compiler_params=pltpu.CompilerParams(collective_id=0, has_side_effects=True, vmem_limit_bytes=30 * 1024 * 1024),
-        )(x_in, act_saved, d_out, w_one, w_two)
+            compiler_params=pltpu.CompilerParams(collective_id=0, has_side_effects=True, vmem_limit_bytes=32 * 1024 * 1024),
+        )(x_in, act_saved, d_out, *(pltpu.with_memory_space_constraint(w, pltpu.HBM) for w in (w_one, w_two)))
 
         depth = 8
         d_x, grad_two, bias = pl.pallas_call(
@@ -467,7 +475,8 @@
             compiler_params=pltpu.CompilerParams(vmem_limit_bytes=14 * 1024 * 1024),
             cost_estimate=pl.CostEstimate(flops=10**10, bytes_accessed=5 * 10**7, transcendentals=0),
         )(packed, grad_two)
-        far = far + lax.ppermute(far, "sp", swap_rows)
+        rest = rest + lax.ppermute(rest, "sp", swap_rows)
+        near, far = jnp.concatenate([near, rest[:third]], axis=0), rest[third:]
         on_left = lax.axis_index("tp") < 2
         grad_one = jnp.concatenate([jnp.where(on_left, near, far), jnp.where(on_left, far, near)], axis=1)
         return d_x.reshape(x_in.shape), grad_one.reshape(w_one.shape), grad_two.reshape(w_two.shape), bias.reshape(half)

time: 756 us -> 753 us (level)
  no operation moved by 1% of the time
where the time goes in v8:
time: 753 us
  Pallas kernels  750 us (100%)
    pallas_call x1, Pallas kernels, local_step(): pl.pallas_call(lambda *refs: body(num, rows, width, *refs), out_shape=(ja...  738 us
  transfers between devices with their start and end apart: 1, of which 0 were waited for; matrix products, arithmetic and copies ran while one was open for 0% of the time, Pallas kernels for 2%

profile of v8, /device:TPU:0, one launch (start us, length us, event | category | flops | bytes accessed | tf_op | source)
XLA Modules:
  0.0 752.9 jit_solution(5452608120912747645)
XLA Ops:
  0.6 737.6 %shard_map.84 = (bf16[32,64,32,128]{3,2,1,0:T(8,128)(2,1)S(1)}, f32[384,128]{1,0:T(8,128)S(1)}, f32[768,128]{1,0:T(8,128)S(1)}, f32[2,584,128]{2,1,0:T(8,128)S(1)}) custom-call(bf16[64,64,32,64]{3,2,1,0:T(8,128)(2,1)} %refs_0_.1, bf16[64,64,32,64]{3,2,1,0:T(8,128)(2,1)} %refs_1_.1, bf16[64,64,32,64]{3,2,1,0:T(8,128)(2,1)} %refs_2_.1, ...), custom_call_target="tpu_custom_call" | custom-call | tf_op jit(solution)/shard_map/pallas_call | solution.py:424
  738.3 0.9 collective-permute-start
  739.2 12.6 %shard_map.85 = (bf16[2,32,64,32,64]{4,3,2,1,0:T(8,128)(2,1)}, f32[576,256]{1,0:T(8,128)}, f32[1,64]{1,0:T(1,128)}) custom-call(bf16[32,64,32,128]{3,2,1,0:T(8,128)(2,1)S(1)} %get-tuple-element.11.refs_0_, f32[2,584,128]{2,1,0:T(8,128)S(1)} %get-tuple-element.12.refs_1_), custom_call_target="tpu_custom_call" | custom-call | flops 10000000000 | bytes 50000000 | tf_op jit(solution)/shard_map/pallas_call | solution.py:461
  751.9 0.0 collective-permute-done
  751.9 0.1 slice_select_fusion.1
  752.0 0.9 pad_maximum_fusion
  (2 shorter events, 0.1 us)
Async XLA Ops:
  738.3 13.6 %collective-permute-start = (f32[768,128]{1,0:T(8,128)S(1)}, f32[768,128]{1,0:T(8,128)S(1)}, u32[]{:S(2)}, u32[]{:S(2)}) collective-permute-start(f32[768,128]{1,0:T(8,128)S(1)} %get-tuple-element.15), channel_id=1, source_target_pairs={{0,4},{4,0},{1,5},{5,1},{2,6},{6,2},{3,7},{7,3}} | collective-permute-start | bytes 1179656 | tf_op jit(solution)/shard_map/ppermute | solution.py:478

commit v9 on v8

--- a/solution.py
+++ b/solution.py
@@ -457,7 +457,7 @@
             compiler_params=pltpu.CompilerParams(collective_id=0, has_side_effects=True, vmem_limit_bytes=32 * 1024 * 1024),
         )(x_in, act_saved, d_out, *(pltpu.with_memory_space_constraint(w, pltpu.HBM) for w in (w_one, w_two)))
 
-        depth = 8
+        depth = 12
         d_x, grad_two, bias = pl.pallas_call(
             lambda *refs: unpack(num, *refs),
             out_shape=(

time: 753 us -> 753 us (level)
  no operation moved by 1% of the time
where the time goes in v9:
time: 753 us
  Pallas kernels  750 us (100%)
    pallas_call x1, Pallas kernels, local_step(): pl.pallas_call(lambda *refs: body(num, rows, width, *refs), out_shape=(ja...  738 us
  transfers between devices with their start and end apart: 1, of which 0 were waited for; matrix products, arithmetic and copies ran while one was open for 0% of the time, Pallas kernels for 2%

profile of v9, /device:TPU:0, one launch (start us, length us, event | category | flops | bytes accessed | tf_op | source)
XLA Modules:
  0.0 753.0 jit_solution(6080674758495218768)
XLA Ops:
  0.6 737.6 %shard_map.84 = (bf16[32,64,32,128]{3,2,1,0:T(8,128)(2,1)S(1)}, f32[384,128]{1,0:T(8,128)S(1)}, f32[768,128]{1,0:T(8,128)S(1)}, f32[2,584,128]{2,1,0:T(8,128)S(1)}) custom-call(bf16[64,64,32,64]{3,2,1,0:T(8,128)(2,1)} %refs_0_.1, bf16[64,64,32,64]{3,2,1,0:T(8,128)(2,1)} %refs_1_.1, bf16[64,64,32,64]{3,2,1,0:T(8,128)(2,1)} %refs_2_.1, ...), custom_call_target="tpu_custom_call" | custom-call | tf_op jit(solution)/shard_map/pallas_call | solution.py:424
  738.3 0.9 collective-permute-start
  739.2 12.8 %shard_map.85 = (bf16[2,32,64,32,64]{4,3,2,1,0:T(8,128)(2,1)}, f32[576,256]{1,0:T(8,128)}, f32[1,64]{1,0:T(1,128)}) custom-call(bf16[32,64,32,128]{3,2,1,0:T(8,128)(2,1)S(1)} %get-tuple-element.11.refs_0_, f32[2,584,128]{2,1,0:T(8,128)S(1)} %get-tuple-element.12.refs_1_), custom_call_target="tpu_custom_call" | custom-call | flops 10000000000 | bytes 50000000 | tf_op jit(solution)/shard_map/pallas_call | solution.py:461
  752.0 0.0 collective-permute-done
  752.1 0.1 slice_select_fusion.1
  752.2 0.9 pad_maximum_fusion
  (2 shorter events, 0.1 us)
Async XLA Ops:
  738.3 13.8 %collective-permute-start = (f32[768,128]{1,0:T(8,128)S(1)}, f32[768,128]{1,0:T(8,128)S(1)}, u32[]{:S(2)}, u32[]{:S(2)}) collective-permute-start(f32[768,128]{1,0:T(8,128)S(1)} %get-tuple-element.15), channel_id=1, source_target_pairs={{0,4},{4,0},{1,5},{5,1},{2,6},{6,2},{3,7},{7,3}} | collective-permute-start | bytes 1179656 | tf_op jit(solution)/shard_map/ppermute | solution.py:478
